TPU v7x, 128 devices: a whole 4x4x4 slice. The times are simulated.
128 devices in a mesh: data: 1, expert: 128 (over z, y, x, core).
Axes of the slice: x: 4, y: 4, z: 4, core: 2. Of those that a mesh axis runs over, the one named last changes fastest.
Arguments:
- tokens: bfloat16 [4096, 2048], P(('data', 'expert'))
- w_router: bfloat16 [2048, 128], replicated
- routes: int32 [4096, 8], P(('data', 'expert'))
- w_gate: bfloat16 [128, 2048, 768], P('expert')
- w_up: bfloat16 [128, 2048, 768], P('expert')
- w_down: bfloat16 [128, 768, 2048], P('expert')
Outputs:
- output: bfloat16 [4096, 2048], P(('data', 'expert'))
All inputs are finite; a program needn't handle non-finite values.
Results may differ from a plain program's by a relative error of at most 0.00817875.
Values are sent between devices in bfloat16 or wider.
A program may use at most 1 GiB of HBM per device.

v0:
```python
import jax
import jax.numpy as jnp
from jax import lax
from jax.sharding import PartitionSpec as P


def solution(mesh):
    group_size = mesh.shape['expert']
    row_spec = P(('data', 'expert'), None)
    expert_spec = P('expert', None, None)

    def device_step(tokens, w_router, routes, w_gate, w_up, w_down):
        tok_count, width = tokens.shape
        slots_per_tok = routes.shape[1]
        experts = w_router.shape[1]
        local_experts = w_gate.shape[0]
        capacity = 4 * tok_count * slots_per_tok // experts
        logits = jnp.dot(tokens, w_router, preferred_element_type=jnp.float32)
        gate_vals = jax.nn.softmax(jnp.take_along_axis(logits, routes, axis=1), axis=-1)
        flat_ids = routes.reshape(-1)
        onehot = (flat_ids[:, None] == jnp.arange(experts, dtype=jnp.int32)[None, :]).astype(jnp.int32)
        pair_rank = jnp.sum((jnp.cumsum(onehot, axis=0) - 1) * onehot, axis=1)
        slot_pos = flat_ids * capacity + pair_rank
        pair_tok = jnp.arange(tok_count * slots_per_tok, dtype=jnp.int32) // slots_per_tok
        slot_tok = jnp.full((experts * capacity,), tok_count, jnp.int32).at[slot_pos].set(pair_tok)
        send_rows = jnp.take(tokens, slot_tok, axis=0, mode='fill', fill_value=0)
        send_rows = send_rows.reshape(group_size, local_experts, capacity, width)
        recv_rows = lax.all_to_all(send_rows, 'expert', 0, 0, tiled=True)
        hidden = jax.nn.silu(jnp.einsum('secd,edf->secf', recv_rows, w_gate, preferred_element_type=jnp.float32)) * jnp.einsum('secd,edf->secf', recv_rows, w_up, preferred_element_type=jnp.float32)
        expert_out = jnp.einsum('secf,efd->secd', hidden.astype(jnp.bfloat16), w_down, preferred_element_type=jnp.float32).astype(jnp.bfloat16)
        back_rows = lax.all_to_all(expert_out, 'expert', 0, 0, tiled=True)
        pair_rows = jnp.take(back_rows.reshape(experts * capacity, width), slot_pos, axis=0)
        pair_rows = pair_rows.reshape(tok_count, slots_per_tok, width)
        combined = jnp.sum(pair_rows * gate_vals[:, :, None], axis=1)
        return combined.astype(jnp.bfloat16)

    return jax.shard_map(device_step, mesh=mesh, in_specs=(row_spec, P(None, None), row_spec, expert_spec, expert_spec, expert_spec), out_specs=row_spec, check_vma=False)
```

profile of v0, /device:TPU:1, one launch (start us, length us, event | category | flops | bytes accessed | tf_op | source)
XLA Modules:
  0.0 190.7 jit_solution(10087662650815591854)
XLA Ops:
  0.0 0.0 copy-start
  0.0 0.0 copy-start.1
  0.0 0.9 copy.20
  0.9 0.1 eq.26
  1.0 0.1 reshape.139
  1.1 0.1 copy.23
  1.2 0.2 fusion.27
  1.5 0.1 add_add_fusion
  1.6 0.1 mul.40
  1.7 0.2 fusion.28
  1.9 1.4 scatter_custom_fusion
  3.3 0.1 broadcast_in_dim.38
  3.4 0.0 copy-done.1
  3.4 6.0 %gather_fusion = bf16[1024,2048]{1,0:T(8,128)(2,1)} fusion(bf16[32,2048]{1,0:T(8,128)(2,1)S(1)} %copy-done.1, s32[1024]{0:T(1024)S(1)} %fusion.33), kind=kCustom, calls=%fused_computation | custom fusion | bytes 8392704 | tf_op jit(solution)/shard_map/jit(_take)/gather | solution.py:26
  9.4 2.5 %fusion.4 = bf16[128,1,8,2048]{3,2,1,0:T(8,128)(2,1)S(1)} fusion(bf16[1024,2048]{1,0:T(8,128)(2,1)} %gather_fusion, pred[128,8]{1,0:T(8,128)(4,1)S(1)} %broadcast_in_dim.38), kind=kLoop, calls=%fused_computation.9 | loop fusion | flops 2097152 | bytes 8389632 | tf_op jit(solution)/shard_map/jit(_take)/select_n | solution.py:26
  12.0 0.0 copy-start.3
  12.0 73.1 %all_to_all.10 = bf16[128,1,8,2048]{3,2,1,0:T(8,128)(2,1)S(1)} all-to-all(bf16[128,1,8,2048]{3,2,1,0:T(8,128)(2,1)S(1)} %fusion.4), channel_id=1, replica_groups=mesh['data'=1,'expert'=128] {'expert'}, dimensions={0} | all-to-all | bytes 8388608 | tf_op jit(solution)/shard_map/all_to_all | solution.py:28
  85.1 0.0 copy-start.2
  85.1 2.0 %copy-done.2 = bf16[128,1,8,2048]{3,2,1,0:T(8,128)(2,1)} copy-done((bf16[128,1,8,2048]{3,2,1,0:T(8,128)(2,1)}, bf16[128,1,8,2048]{3,2,1,0:T(8,128)(2,1)S(1)}, u32[]{:S(2)}) %copy-start.2) | copy-done | bytes 4194328
  87.1 0.0 copy-done.3
  87.1 9.8 %fusion.2 = f32[128,8,768]{2,0,1:T(8,128)} fusion(bf16[128,1,8,2048]{3,2,1,0:T(8,128)(2,1)S(1)} %all_to_all.10, bf16[1,2048,768]{2,1,0:T(8,128)(2,1)S(1)} %copy-done.3), kind=kOutput, calls=%fused_computation.6 | convolution fusion | flops 3221225472 | bytes 10485760 | tf_op jit(solution)/shard_map/secd,edf->secf/dot_general | solution.py:29
  96.9 0.0 copy-done
  96.9 14.6 %convert_bitcast_fusion = bf16[128,1,8,2048]{3,0,2,1:T(8,128)(2,1)} fusion(bf16[1,768,2048]{2,1,0:T(8,128)(2,1)S(1)} %copy-done, f32[128,8,768]{2,0,1:T(8,128)} %fusion.2, bf16[1,2048,768]{2,1,0:T(8,128)(2,1)} %param.10, bf16[128,1,8,2048]{3,2,1,0:T(8,128)(2,1)} %copy-done.2), kind=kOutput, calls=%fused_computation.10 | convolution fusion | flops 6449266688 | bytes 17825792 | tf_op jit(solution)/shard_map/secf,efd->secd/dot_general | solution.py:30
  111.4 6.5 %copy.27 = bf16[128,1,8,2048]{3,2,1,0:T(8,128)(2,1)} copy(bf16[128,1,8,2048]{3,0,2,1:T(8,128)(2,1)} %convert_bitcast_fusion) | data formatting | bytes 8388608 | tf_op jit(solution)/shard_map/convert_element_type | solution.py:30
  117.9 4.8 %all-to-all-start.1 = ((bf16[128,1,8,2048]{3,2,1,0:T(8,128)(2,1)}), bf16[128,1,8,2048]{3,2,1,0:T(8,128)(2,1)}, u32[]{:S(2)}, u32[]{:S(2)}) async-start(bf16[128,1,8,2048]{3,2,1,0:T(8,128)(2,1)} %copy.27), calls=%async_computation.1 | async-start | bytes 8388608 | tf_op jit(solution)/shard_map/all_to_all | solution.py:31
  122.7 0.1 reduce_sum.32
  122.8 0.1 reshape.164
  122.9 1.2 fusion.38
  124.1 1.9 gather_fusion.2
  126.0 0.1 reshape.167
  126.1 0.1 fusion.37
  126.2 0.2 fusion.32
  126.4 0.1 fusion.31
  126.5 54.8 %all-to-all-done.1 = bf16[128,1,8,2048]{3,2,1,0:T(8,128)(2,1)} async-done(((bf16[128,1,8,2048]{3,2,1,0:T(8,128)(2,1)}), bf16[128,1,8,2048]{3,2,1,0:T(8,128)(2,1)}, u32[]{:S(2)}, u32[]{:S(2)}) %all-to-all-start.1) | async-done | bytes 4194336 | tf_op jit(solution)/shard_map/all_to_all | solution.py:31
  181.3 6.1 %gather_fusion.1 = bf16[256,2048]{1,0:T(8,128)(2,1)} fusion(bf16[1024,2048]{1,0:T(8,128)(2,1)} %bitcast.26, s32[1024]{0:T(1024)S(1)} %pad_clamp_fusion), kind=kCustom, calls=%fused_computation.1 | custom fusion | bytes 2098176 | tf_op jit(solution)/shard_map/jit(_take)/gather | solution.py:32
  187.4 3.3 %multiply_reduce_fusion = bf16[32,2048]{1,0:T(8,128)(2,1)} fusion(bf16[256,2048]{1,0:T(8,128)(2,1)} %gather_fusion.1, f32[32,8]{1,0:T(8,128)S(1)} %fusion.31, pred[32,8]{1,0:T(8,128)(4,1)S(1)} %compare_and_fusion), kind=kLoop, calls=%fused_computation.23 | loop fusion | flops 2031616 | bytes 1180928 | tf_op jit(solution)/shard_map/reduce_sum | solution.py:34
  (12 shorter events, 0.1 us)
Async XLA Ops:
  0.0 96.9 %copy-start = (bf16[1,768,2048]{2,1,0:T(8,128)(2,1)S(1)}, bf16[1,768,2048]{2,1,0:T(8,128)(2,1)}, u32[]{:S(2)}) copy-start(bf16[1,768,2048]{2,1,0:T(8,128)(2,1)} %param.11) | copy-start | bytes 9437188
  0.0 3.4 %copy-start.1 = (bf16[32,2048]{1,0:T(8,128)(2,1)S(1)}, bf16[32,2048]{1,0:T(8,128)(2,1)}, u32[]{:S(2)}) copy-start(bf16[32,2048]{1,0:T(8,128)(2,1)} %param.6) | copy-start | bytes 393220
  12.0 75.1 %copy-start.3 = (bf16[1,2048,768]{2,1,0:T(8,128)(2,1)S(1)}, bf16[1,2048,768]{2,1,0:T(8,128)(2,1)}, u32[]{:S(2)}) copy-start(bf16[1,2048,768]{2,1,0:T(8,128)(2,1)} %param.9) | copy-start | bytes 9437188
  85.1 2.0 %copy-start.2 = (bf16[128,1,8,2048]{3,2,1,0:T(8,128)(2,1)}, bf16[128,1,8,2048]{3,2,1,0:T(8,128)(2,1)S(1)}, u32[]{:S(2)}) copy-start(bf16[128,1,8,2048]{3,2,1,0:T(8,128)(2,1)S(1)} %all_to_all.10) | copy-start | bytes 12582916
  117.9 63.4 %all-to-all-start.1 = ((bf16[128,1,8,2048]{3,2,1,0:T(8,128)(2,1)}), bf16[128,1,8,2048]{3,2,1,0:T(8,128)(2,1)}, u32[]{:S(2)}, u32[]{:S(2)}) async-start(bf16[128,1,8,2048]{3,2,1,0:T(8,128)(2,1)} %copy.27), calls=%async_computation.1 | async-start | bytes 8388608 | tf_op jit(solution)/shard_map/all_to_all | solution.py:31
where the time goes:
time: 192 us; the launch traced here: 191 us
  blocking collectives  73.1 us (38%)
  waiting for transfers between devices  54.8 us (29%)
  matrix products  25.6 us (13%)
  local copies, waits for them, and re-layouts  25.5 us (13%)
  other arithmetic  6.8 us (4%)
  starting transfers between devices  4.79 us (2%)
    all_to_all x1, blocking collectives, device_step(): recv_rows = lax.all_to_all(send_rows, 'expert', 0, 0, tiled=True)  73.1 us
    all_to_all x1, waiting for transfers between devices, device_step(): back_rows = lax.all_to_all(expert_out, 'expert', 0, 0, tiled=True)  54.8 us
    dot_general x1, matrix products, device_step(): jnp.einsum('secf,efd->secd', hidden.astype(jnp.bfloat16), w_down, preferr...  14.6 us
    dot_general x1, matrix products, device_step(): jnp.einsum('secd,edf->secf', recv_rows, w_gate, preferred_element_type=jn...  9.78 us
    convert_element_type x1, local copies, waits for them, and re-layouts, device_step(): jnp.einsum('secf,efd->secd', hidden.astype(jnp.bfloat16), w_down, preferr...  6.45 us
    gather x1, local copies, waits for them, and re-layouts, device_step(): jnp.take(back_rows.reshape(experts * capacity, width), slot_pos, axis=0)  6.06 us
    gather x1, local copies, waits for them, and re-layouts, device_step(): send_rows = jnp.take(tokens, slot_tok, axis=0, mode='fill', fill_value=0)  6.02 us
    all_to_all x1, starting transfers between devices, device_step(): back_rows = lax.all_to_all(expert_out, 'expert', 0, 0, tiled=True)  4.79 us
  transfers between devices with their start and end apart: 1, of which 1 were waited for; matrix products, arithmetic and copies ran while one was open for 2% of the time, Pallas kernels for 0%

commit v1 on v0

v1 whole, which is shorter than its diff:
```python
import functools

import jax
import jax.numpy as jnp
from jax import lax
from jax.experimental import pallas as pl
from jax.experimental.pallas import tpu as pltpu
from jax.sharding import PartitionSpec as P

F32 = jnp.float32
BF16 = jnp.bfloat16
CAP = 8


def _iota(shape, dim):
    return lax.broadcasted_iota(jnp.int32, shape, dim)


def prep_kernel(x_ref, wr_ref, r_ref, tab_ref, aux_ref):
    tok, experts = x_ref.shape[0], wr_ref.shape[1]
    logits = jnp.dot(x_ref[...], wr_ref[...], preferred_element_type=F32)
    routes = r_ref[...]
    lane = _iota((tok, experts), 1)
    hit = jnp.zeros((tok, experts), F32)
    for j in range(routes.shape[1]):
        hit += (routes[:, j:j + 1] == lane).astype(F32)
    on = hit > 0.5
    masked = jnp.where(on, logits, -jnp.inf)
    top = jnp.max(masked, axis=1, keepdims=True)
    e = jnp.where(on, jnp.exp(jnp.where(on, logits, top) - top), 0.0)
    gate = e / jnp.sum(e, axis=1, keepdims=True)
    below = (_iota((tok, tok), 1) < _iota((tok, tok), 0)).astype(BF16)
    rank = jnp.dot(below, hit.astype(BF16), preferred_element_type=F32)
    rank = jnp.where(on, rank, -1.0)
    row = _iota((tok, experts), 0).astype(F32)
    rows = []
    for r in range(CAP):
        rows.append(jnp.sum(jnp.where(rank == r, row + 1.0, 0.0), axis=0, keepdims=True) - 1.0)
    tab_ref[...] = jnp.concatenate(rows, axis=0)
    g1 = gate.astype(BF16)
    rest = gate - g1.astype(F32)
    g2 = rest.astype(BF16)
    g3 = (rest - g2.astype(F32)).astype(BF16)
    aux_ref[...] = jnp.concatenate([g1, g2, g3, rank.astype(BF16)], axis=0)


def ffn_kernel(tab_ref, x_ref, wg_ref, wu_ref, wd_ref, o_ref, rows_ref):
    me = lax.axis_index('expert')
    n_rows = tab_ref.shape[0]
    tab = tab_ref[...]
    col = jnp.sum(jnp.where(_iota(tab.shape, 1) == me, tab, 0.0), axis=1, keepdims=True)
    for g in range(n_rows // 64):
        c = col[g * 64:(g + 1) * 64]
        src = (_iota((64, 1), 0) // CAP * 32).astype(F32)
        want = jnp.where(c >= 0.0, c + src, -1.0)
        pick = (want == _iota((64, 256), 1).astype(F32)).astype(BF16)
        rows_ref[g * 64:(g + 1) * 64] = jnp.dot(pick, x_ref[g * 256:(g + 1) * 256], preferred_element_type=F32).astype(BF16)
    rows = rows_ref[...]
    a = jnp.dot(rows, wg_ref[...], preferred_element_type=F32)
    b = jnp.dot(rows, wu_ref[...], preferred_element_type=F32)
    h = (a * jax.nn.sigmoid(a) * b).astype(BF16)
    o_ref[...] = jnp.dot(h, wd_ref[...], preferred_element_type=F32).astype(BF16)


def combine_kernel(aux_ref, back_ref, y_ref, gate_ref):
    tok = y_ref.shape[0]
    experts = aux_ref.shape[1]
    slots = back_ref.shape[0]

    @pl.when(pl.program_id(0) == 0)
    def _():
        spread = (_iota((experts, slots), 1) // CAP == _iota((experts, slots), 0)).astype(BF16)
        wide = jnp.dot(aux_ref[...], spread, preferred_element_type=F32)
        here = wide[3 * tok:] == (_iota((tok, slots), 1) % CAP).astype(F32)
        for p in range(3):
            gate_ref[p * tok:(p + 1) * tok] = jnp.where(here, wide[p * tok:(p + 1) * tok], 0.0).astype(BF16)

    y = jnp.dot(gate_ref[...], back_ref[...], preferred_element_type=F32)
    y_ref[...] = (y[:tok] + y[tok:2 * tok] + y[2 * tok:]).astype(BF16)


def solution(mesh):
    row_spec = P(('data', 'expert'), None)
    expert_spec = P('expert', None, None)
    vmem = pl.BlockSpec(memory_space=pltpu.VMEM)

    def device_step(tokens, w_router, routes, w_gate, w_up, w_down):
        tok, width = tokens.shape
        experts = w_router.shape[1]
        ff = w_gate.shape[2]
        slots = experts * CAP
        tab, aux = pl.pallas_call(
            prep_kernel,
            out_shape=(jax.ShapeDtypeStruct((CAP, experts), F32), jax.ShapeDtypeStruct((4 * tok, experts), BF16)),
            in_specs=[vmem] * 3, out_specs=(vmem, vmem), name='prep',
        )(tokens, w_router, routes)
        all_x = lax.all_gather(tokens, 'expert', axis=0, tiled=True)
        all_tab = lax.all_gather(tab, 'expert', axis=0, tiled=True)
        steps = 4
        m, k = slots // steps, experts * tok // steps
        out = pl.pallas_call(
            ffn_kernel,
            grid=(steps,),
            out_shape=jax.ShapeDtypeStruct((slots, width), BF16),
            in_specs=[
                pl.BlockSpec((m, experts), lambda i: (i, 0)),
                pl.BlockSpec((k, width), lambda i: (i, 0)),
                pl.BlockSpec((None, width, ff), lambda i: (0, 0, 0), pipeline_mode=pl.Buffered(1)),
                pl.BlockSpec((None, width, ff), lambda i: (0, 0, 0), pipeline_mode=pl.Buffered(1)),
                pl.BlockSpec((None, ff, width), lambda i: (0, 0, 0), pipeline_mode=pl.Buffered(1)),
            ],
            out_specs=pl.BlockSpec((m, width), lambda i: (i, 0)),
            scratch_shapes=[pltpu.VMEM((m, width), BF16)],
            name='ffn',
        )(all_tab, all_x, w_gate, w_up, w_down)
        back = lax.all_to_all(out.reshape(experts, CAP, width), 'expert', 0, 0, tiled=True).reshape(slots, width)
        nt = 512
        return pl.pallas_call(
            combine_kernel,
            grid=(width // nt,),
            out_shape=jax.ShapeDtypeStruct((tok, width), BF16),
            in_specs=[pl.BlockSpec((4 * tok, experts), lambda i: (0, 0)), pl.BlockSpec((slots, nt), lambda i: (0, i))],
            out_specs=pl.BlockSpec((tok, nt), lambda i: (0, i)),
            scratch_shapes=[pltpu.VMEM((3 * tok, slots), BF16)],
            name='combine',
        )(aux, back)

    return jax.shard_map(device_step, mesh=mesh, in_specs=(row_spec, P(None, None), row_spec, expert_spec, expert_spec, expert_spec), out_specs=row_spec, check_vma=False)
```

time: 192 us -> 193 us (level)
  blocking collectives: 73.1 us -> 107 us
  Pallas kernels: 0 us -> 26.3 us
  matrix products: 25.6 us -> 0 us
  local copies, waits for them, and re-layouts: 25.5 us -> 1.37 us
  between operations: 0.17 us -> 13.4 us
  waiting for transfers between devices: 54.8 us -> 43.6 us
  other arithmetic: 6.8 us -> 0 us
  starting transfers between devices: 4.79 us -> 0.01 us
    all_to_all x1 -> x0, waiting for transfers between devices: 54.8 us -> none  [device_step(): back_rows = lax.all_to_all(expert_out, 'expert', 0, 0, tiled=True)]
    all_gather x0 -> x1, waiting for transfers between devices: none -> 42.9 us  [device_step(): all_x = lax.all_gather(tokens, 'expert', axis=0, tiled=True)]
    all_gather x0 -> x1, blocking collectives: none -> 40.2 us  [device_step(): all_tab = lax.all_gather(tab, 'expert', axis=0, tiled=True)]
    pallas_call x0 -> x3, Pallas kernels: none -> 26.3 us  [the longest x1 19.7 us: device_step(): pl.pallas_call(ffn_kernel, grid=(steps,), out_shape=jax.ShapeDtypeStruct(...]
    dot_general x3 -> x0, matrix products: 25.6 us -> none  [the longest x1 14.6 us: device_step(): jnp.einsum('secf,efd->secd', hidden.astype(jnp.bfloat16), w_down, preferr...]
    gather x5 -> x0, local copies, waits for them, and re-layouts: 14.2 us -> none  [the longest x1 6.06 us: device_step(): jnp.take(back_rows.reshape(experts * capacity, width), slot_pos, axis=0)]
    all_to_all x1, blocking collectives: 73.1 us -> 66.4 us  [device_step(): lax.all_to_all(out.reshape(experts, CAP, width), 'expert', 0, 0, tiled=True)]
    convert_element_type x1 -> x0, local copies, waits for them, and re-layouts: 6.45 us -> none  [device_step(): jnp.einsum('secf,efd->secd', hidden.astype(jnp.bfloat16), w_down, preferr...]
  transfers between devices with their start and end apart: 1 -> 1, of which waited for: 1 -> 1; matrix products, arithmetic and copies ran while one was open for 2% -> 1% of each run, Pallas kernels for 0% -> 1%
where the time goes in v1:
time: 193 us; the launch traced here: 191 us
  blocking collectives  107 us (55%)
  waiting for transfers between devices  43.6 us (23%)
  Pallas kernels  26.3 us (14%)
  between operations  13.4 us (7%)
    all_to_all x1, blocking collectives, device_step(): lax.all_to_all(out.reshape(experts, CAP, width), 'expert', 0, 0, tiled=True)  66.4 us
    all_gather x1, waiting for transfers between devices, device_step(): all_x = lax.all_gather(tokens, 'expert', axis=0, tiled=True)  42.9 us
    all_gather x1, blocking collectives, device_step(): all_tab = lax.all_gather(tab, 'expert', axis=0, tiled=True)  40.2 us
    pallas_call x1, Pallas kernels, device_step(): pl.pallas_call(ffn_kernel, grid=(steps,), out_shape=jax.ShapeDtypeStruct(...  19.7 us
    pallas_call x1, Pallas kernels, device_step(): pl.pallas_call(combine_kernel, grid=(width // nt,), out_shape=jax.ShapeDt...  4.58 us
  transfers between devices with their start and end apart: 1, of which 1 were waited for; matrix products, arithmetic and copies ran while one was open for 1% of the time, Pallas kernels for 1%

profile of v1, /device:TPU:1, one launch (start us, length us, event | category | flops | bytes accessed | tf_op | source)
XLA Modules:
  0.0 191.4 jit_solution(6797062300343446551)
XLA Ops:
  6.5 0.0 all-gather.2.cloned.1.call-start
  6.5 0.7 all-gather.2.cloned.1.call-update
  7.3 1.4 copy.7.r_ref
  8.6 2.0 %prep.1 = (f32[8,128]{1,0:T(8,128)}, bf16[128,128]{1,0:T(8,128)(2,1)}) custom-call(bf16[32,2048]{1,0:T(8,128)(2,1)} %x_ref.1, bf16[2048,128]{1,0:T(8,128)(2,1)} %wr_ref.1, s32[32,8]{1,0:T(8,128)} %copy.7.r_ref), custom_call_target="tpu_custom_call" | custom-call | tf_op jit(solution)/shard_map/prep/pallas_call | solution.py:92
  10.7 40.2 %all_gather.6.tab_ref = f32[1024,128]{1,0:T(8,128)} all-gather(f32[8,128]{1,0:T(8,128)} %get-tuple-element.8), channel_id=1, replica_groups=mesh['data'=1,'expert'=128] {'expert'}, dimensions={0}, use_global_device_ids=true | all-gather | bytes 528384 | tf_op jit(solution)/shard_map/all_gather | solution.py:98
  50.9 42.9 %all-gather.2.cloned.1.call-done.x_ref = bf16[4096,2048]{1,0:T(8,128)(2,1)} async-done(((bf16[32,2048]{1,0:T(8,128)(2,1)}), bf16[4096,2048]{1,0:T(8,128)(2,1)}) %all-gather.2.cloned.1.call-update) | async-done | bytes 16777232 | tf_op jit(solution)/shard_map/all_gather | solution.py:97
  93.8 19.7 %ffn.1 = bf16[1024,2048]{1,0:T(8,128)(2,1)} custom-call(f32[1024,128]{1,0:T(8,128)} %all_gather.6.tab_ref, bf16[4096,2048]{1,0:T(8,128)(2,1)} %all-gather.2.cloned.1.call-done.x_ref, bf16[1,2048,768]{2,1,0:T(8,128)(2,1)} %wg_ref.1, bf16[1,2048,768]{2,1,0:T(8,128)(2,1)} %wu_ref.1, bf16[1,768,2048]{2,1,0:T(8,128)(2,1)} %wd_ref.1), custom_call_target="tpu_custom_call" | custom-call | tf_op jit(solution)/shard_map/ffn/pallas_call | solution.py:101
  113.5 66.4 %all_to_all.5 = bf16[128,8,2048]{2,1,0:T(8,128)(2,1)} all-to-all(bf16[128,8,2048]{2,1,0:T(8,128)(2,1)} %bitcast.3), channel_id=1, replica_groups=mesh['data'=1,'expert'=128] {'expert'}, dimensions={0} | all-to-all | bytes 8388608 | tf_op jit(solution)/shard_map/all_to_all | solution.py:116
  179.9 4.6 %combine.1 = bf16[32,2048]{1,0:T(8,128)(2,1)} custom-call(bf16[128,128]{1,0:T(8,128)(2,1)} %get-tuple-element.7.aux_ref, bf16[1024,2048]{1,0:T(8,128)(2,1)} %bitcast.2), custom_call_target="tpu_custom_call" | custom-call | tf_op jit(solution)/shard_map/combine/pallas_call | solution.py:118
Async XLA Ops:
  6.5 87.2 %all-gather.2.cloned.1.call-start = ((), (), s32[]{:S(2)}) async-start(), calls=%async_computation.1 | async-start | bytes 16908288 | tf_op jit(solution)/shard_map/all_gather | solution.py:97
Sparse Core Ops, SparseCore 0:
  10.5 83.2 all-gather.1

commit v2 on v0

v2 whole, which is shorter than its diff:
```python
import functools

import jax
import jax.numpy as jnp
from jax import lax
from jax.experimental import pallas as pl
from jax.experimental.pallas import tpu as pltpu
from jax.sharding import PartitionSpec as P

F32 = jnp.float32
BF16 = jnp.bfloat16
CAP = 8
ORDERS = ((2, 1, 0), (1, 0, 2), (0, 2, 1))


def _iota(shape, dim):
    return lax.broadcasted_iota(jnp.int32, shape, dim)


def prep_kernel(x_ref, wr_ref, r_ref, tab_ref):
    tok, experts = x_ref.shape[0], wr_ref.shape[1]
    logits = jnp.dot(x_ref[...], wr_ref[...], preferred_element_type=F32)
    routes = r_ref[...]
    lane = _iota((tok, experts), 1)
    hit = jnp.zeros((tok, experts), F32)
    for j in range(routes.shape[1]):
        hit += (routes[:, j:j + 1] == lane).astype(F32)
    on = hit > 0.5
    masked = jnp.where(on, logits, -jnp.inf)
    top = jnp.max(masked, axis=1, keepdims=True)
    e = jnp.where(on, jnp.exp(jnp.where(on, logits, top) - top), 0.0)
    gate = e / jnp.sum(e, axis=1, keepdims=True)
    below = (_iota((tok, tok), 1) < _iota((tok, tok), 0)).astype(BF16)
    rank = jnp.dot(below, hit.astype(BF16), preferred_element_type=F32)
    rank = jnp.where(on, rank, -1.0)
    row = _iota((tok, experts), 0).astype(F32)
    toks, gates = [], []
    for r in range(CAP):
        at = rank == r
        toks.append(jnp.sum(jnp.where(at, row + 1.0, 0.0), axis=0, keepdims=True) - 1.0)
        gates.append(jnp.sum(jnp.where(at, gate, 0.0), axis=0, keepdims=True))
    tab_ref[...] = jnp.concatenate(toks + gates, axis=0)


def moe_kernel(n, parts, x_ref, tab_ref, wg_hbm, wu_hbm, wd_hbm, y_ref, wg, wu, wd, rbuf, obuf, *rest):
    np_ = len(parts)
    tbuf, xbuf, sbuf, cbuf, bbuf, pbuf, abuf = [rest[i * np_:(i + 1) * np_] for i in range(7)]
    (w_sem, ta_s, ta_r, tb_s, tb_r, xa_s, xa_r, xb_s, xb_r, c_s, c_r, rc_s, rc_r, rb_s, rb_r, ra_s, ra_r) = rest[7 * np_:]
    tok = x_ref.shape[0]
    experts = tab_ref.shape[1]
    me = lax.axis_index('expert')
    strides = (2 * n * n, 2 * n, 2)
    pos = tuple(lax.rem(me // s, n) for s in strides)
    core = lax.rem(me, 2)

    def moved(axis, d, flip=0):
        other = me + (lax.rem(pos[axis] + d, n) - pos[axis]) * strides[axis]
        return other + (1 - 2 * core) if flip else other

    def put(src, dst, send, recv, device):
        pltpu.make_async_remote_copy(src_ref=src, dst_ref=dst, send_sem=send, recv_sem=recv,
                                     device_id={'expert': device}, device_id_type=pl.DeviceIdType.MESH).start()

    def drain(ref, sem):
        pltpu.make_async_copy(ref, ref, sem).wait()

    loads = [pltpu.make_async_copy(src, dst, w_sem.at[i]) for i, (src, dst) in enumerate(((wg_hbm.at[0], wg), (wu_hbm.at[0], wu), (wd_hbm.at[0], wd)))]
    for load in loads:
        load.start()

    barrier = pltpu.get_barrier_semaphore()
    peers = [moved(axis, d, flip) for axis in range(3) for d in range(1, n) for flip in (0, 1)] + [moved(0, 0, 1)]
    for peer in peers:
        pl.semaphore_signal(barrier, inc=1, device_id={'expert': peer}, device_id_type=pl.DeviceIdType.MESH)
    pl.semaphore_wait(barrier, len(peers))

    def canon(ref, p, a, b, k, c):
        axes = ORDERS[p]
        index = [None] * 3
        index[axes[0]], index[axes[1]], index[axes[2]] = a, b, k
        off, w = parts[p]
        return ref.at[index[0], index[1], index[2], c, :, pl.ds(off, w)]

    every = pl.ds(0, n)
    at = [tuple(pos[axis] for axis in ORDERS[p]) for p in range(np_)]

    for p in range(np_):
        a, b, _ = at[p]
        for d in range(1, n):
            put(tab_ref, tbuf[p].at[b, a], ta_s.at[p], ta_r.at[p], moved(ORDERS[p][0], d))
    for d in range(1, n):
        for p in range(np_):
            a, b, _ = at[p]
            off, w = parts[p]
            put(x_ref.at[:, pl.ds(off, w)], xbuf[p].at[b, a], xa_s.at[p], xa_r.at[p, d - 1], moved(ORDERS[p][0], d))
    for d in range(1, n):
        for p in range(np_):
            a, b, _ = at[p]
            off, w = parts[p]
            put(x_ref.at[:, pl.ds(off, w)], xbuf[p].at[b, a], xb_s.at[p], xb_r.at[p, d - 1], moved(ORDERS[p][1], d))
    for p in range(np_):
        a, b, _ = at[p]
        off, w = parts[p]
        xbuf[p][b, a] = x_ref[:, off:off + w]
        tbuf[p][b, a] = tab_ref[...]
    for p in range(np_):
        a, b, _ = at[p]
        drain(tbuf[p].at[0, pl.ds(0, n - 1)], ta_r.at[p])
        for d in range(1, n):
            put(tbuf[p].at[b], tbuf[p].at[b], tb_s.at[p], tb_r.at[p], moved(ORDERS[p][1], d))
    for da in range(1, n):
        for p in range(np_):
            a, b, _ = at[p]
            src = lax.rem(a + n - da, n)
            drain(xbuf[p].at[0, 0], xa_r.at[p, da - 1])
            for d in range(1, n):
                put(xbuf[p].at[b, src], xbuf[p].at[b, src], xb_s.at[p], xb_r.at[p, d - 1], moved(ORDERS[p][1], d))
    for db in range(n):
        for p in range(np_):
            a, b, k = at[p]
            axis_c = ORDERS[p][2]
            off, w = parts[p]
            bb = lax.rem(b + n - db, n)
            if db == 1:
                drain(tbuf[p].at[pl.ds(0, n - 1)], tb_r.at[p])
            if db:
                drain(xbuf[p].at[0], xb_r.at[p, db - 1])
            table = tbuf[p][bb][:, :CAP].reshape(n * CAP, experts)
            shift = (_iota((n * CAP, 1), 0) // CAP * tok).astype(F32)
            lane = _iota((n * CAP, experts), 1)
            token = _iota((n * CAP, n * tok), 1).astype(F32)
            picks = []
            for dk in range(n):
                for flip in range(2):
                    col = jnp.sum(jnp.where(lane == moved(axis_c, dk, flip), table, 0.0), axis=1, keepdims=True)
                    want = jnp.where(col >= 0.0, col + shift, -1.0)
                    picks.append((want == token).astype(F32))
            pick = jnp.concatenate(picks, axis=0).astype(BF16)
            rows = jnp.dot(pick, xbuf[p][bb].reshape(n * tok, w), preferred_element_type=F32).astype(BF16)
            rows = rows.reshape(2 * n, n, CAP, w)
            sbuf[p][db] = rows
            index = [None] * 3
            index[ORDERS[p][0]], index[ORDERS[p][1]], index[axis_c] = slice(None), bb, k
            rbuf[index[0], index[1], index[2], core, :, off:off + w] = rows[0]
            for q in range(1, 2 * n):
                put(sbuf[p].at[db, q], canon(rbuf, p, every, bb, k, core), c_s.at[p], c_r.at[p], moved(axis_c, q // 2, q % 2))

    for load in loads:
        load.wait()
    for p in range(np_):
        drain(sbuf[p].at[:, pl.ds(0, 2 * n - 1)], c_r.at[p])

    def expert(i, carry):
        rows = rbuf[i].reshape(n * n * 2 * CAP, x_ref.shape[1])
        g = jnp.dot(rows, wg[...], preferred_element_type=F32)
        u = jnp.dot(rows, wu[...], preferred_element_type=F32)
        h = (g * jax.nn.sigmoid(g) * u).astype(BF16)
        o = jnp.dot(h, wd[...], preferred_element_type=F32).astype(BF16)
        obuf[i] = o.reshape(n, n, 2, CAP, x_ref.shape[1])
        return carry

    lax.fori_loop(0, n, expert, 0)

    for db in range(n):
        for p in range(np_):
            a, b, k = at[p]
            axis_c = ORDERS[p][2]
            off, w = parts[p]
            bb = lax.rem(b + db, n)
            mine = k * 2 + core
            for q in range(1, 2 * n):
                dk, flip = q // 2, q % 2
                there = lax.rem(k + dk, n)
                c = 1 - core if flip else core
                put(canon(obuf, p, every, bb, there, c), cbuf[p].at[bb, :, mine], rc_s.at[p], rc_r.at[p, (n - db) % n], moved(axis_c, dk, flip))
            index = [None] * 3
            index[ORDERS[p][0]], index[ORDERS[p][1]], index[axis_c] = slice(None), bb, k
            cbuf[p][bb, :, mine] = obuf[index[0], index[1], index[2], core, :, off:off + w]
    for db in list(range(1, n)) + [0]:
        for p in range(np_):
            a, b, _ = at[p]
            bb = lax.rem(b + db, n)
            drain(cbuf[p].at[0, :, pl.ds(0, 2 * n - 1)], rc_r.at[p, (n - db) % n])
            if db:
                put(cbuf[p].at[bb], bbuf[p].at[:, b], rb_s.at[p], rb_r.at[p], moved(ORDERS[p][1], db))
            else:
                bbuf[p][:, b] = cbuf[p][b]
    cols = n * 2 * n * CAP
    for p in range(np_):
        a, b, k = at[p]
        axis_a, axis_b, axis_c = ORDERS[p]
        off, w = parts[p]
        drain(cbuf[p].at[pl.ds(0, n - 1)], rb_r.at[p])
        slot = _iota((experts, cols), 1)
        ident = (slot // (2 * n * CAP) * strides[axis_b] + lax.rem(slot // (2 * CAP), n) * strides[axis_c]
                 + lax.rem(slot // CAP, 2) + a * strides[axis_a])
        spread = (ident == _iota((experts, cols), 0)).astype(BF16)
        keep = _iota((CAP, cols), 0) == lax.rem(_iota((CAP, cols), 1), CAP)
        for da in list(range(1, n)) + [0]:
            aa = lax.rem(a + da, n)
            tg = tbuf[p][b, aa]
            gate = tg[CAP:]
            g1 = gate.astype(BF16).astype(F32)
            g2 = (gate - g1).astype(BF16).astype(F32)
            g3 = gate - g1 - g2
            wide = jnp.dot(jnp.concatenate([tg[:CAP], g1, g2, g3], axis=0).astype(BF16), spread, preferred_element_type=F32)
            line = [jnp.sum(jnp.where(keep, wide[i * CAP:(i + 1) * CAP], 0.0), axis=0, keepdims=True) for i in range(4)]
            here = line[0] == _iota((tok, cols), 0).astype(F32)
            mix = jnp.concatenate([jnp.where(here, line[i], 0.0) for i in (1, 2, 3)], axis=0).astype(BF16)
            part = jnp.dot(mix, bbuf[p][aa].reshape(cols, w), preferred_element_type=F32)
            part = part[:tok] + part[tok:2 * tok] + part[2 * tok:]
            if da:
                pbuf[p][da - 1] = part
                put(pbuf[p].at[da - 1], abuf[p].at[a], ra_s.at[p], ra_r.at[p], moved(axis_a, da))
            else:
                abuf[p][a] = part
    for p in range(np_):
        off, w = parts[p]
        drain(pbuf[p], ra_r.at[p])
        total = abuf[p][0]
        for i in range(1, n):
            total += abuf[p][i]
        y_ref[:, off:off + w] = total.astype(BF16)
    for p in range(np_):
        drain(tbuf[p].at[0, pl.ds(0, n - 1)], ta_s.at[p])
        drain(tbuf[p].at[pl.ds(0, n - 1)], tb_s.at[p])
        drain(xbuf[p].at[0, pl.ds(0, n - 1)], xa_s.at[p])
        drain(xbuf[p].at[pl.ds(0, n - 1)], xb_s.at[p])
        drain(sbuf[p].at[:, pl.ds(0, 2 * n - 1)], c_s.at[p])
        drain(cbuf[p].at[:, :, pl.ds(0, 2 * n - 1)], rc_s.at[p])
        drain(cbuf[p].at[pl.ds(0, n - 1)], rb_s.at[p])
        drain(pbuf[p], ra_s.at[p])


def build(mesh, n, parts):
    row_spec = P(('data', 'expert'), None)
    expert_spec = P('expert', None, None)
    vmem = pl.BlockSpec(memory_space=pltpu.VMEM)
    hbm = pl.BlockSpec(memory_space=pl.ANY)

    def device_step(tokens, w_router, routes, w_gate, w_up, w_down):
        tok, width = tokens.shape
        experts = w_router.shape[1]
        ff = w_gate.shape[2]
        tab = pl.pallas_call(
            prep_kernel, out_shape=jax.ShapeDtypeStruct((2 * CAP, experts), F32),
            in_specs=[vmem] * 3, out_specs=vmem, name='prep',
        )(tokens, w_router, routes)
        dma = pltpu.SemaphoreType.DMA
        np_ = len(parts)
        return pl.pallas_call(
            functools.partial(moe_kernel, n, parts),
            out_shape=jax.ShapeDtypeStruct((tok, width), BF16),
            in_specs=[vmem, vmem, hbm, hbm, hbm], out_specs=vmem,
            scratch_shapes=[
                pltpu.VMEM((width, ff), BF16), pltpu.VMEM((width, ff), BF16), pltpu.VMEM((ff, width), BF16),
                pltpu.VMEM((n, n, n, 2, CAP, width), BF16), pltpu.VMEM((n, n, n, 2, CAP, width), BF16),
                *[pltpu.VMEM((n, n, 2 * CAP, experts), F32) for _ in parts],
                *[pltpu.VMEM((n, n, tok, w), BF16) for _, w in parts],
                *[pltpu.VMEM((n, 2 * n, n, CAP, w), BF16) for _, w in parts],
                *[pltpu.VMEM((n, n, 2 * n, CAP, w), BF16) for _, w in parts],
                *[pltpu.VMEM((n, n, 2 * n, CAP, w), BF16) for _, w in parts],
                *[pltpu.VMEM((n - 1, tok, w), F32) for _, w in parts],
                *[pltpu.VMEM((n, tok, w), F32) for _, w in parts],
                dma((3,)), dma((np_,)), dma((np_,)), dma((np_,)), dma((np_,)),
                dma((np_,)), dma((np_, n - 1)), dma((np_,)), dma((np_, n - 1)), dma((np_,)), dma((np_,)),
                dma((np_,)), dma((np_, n)), dma((np_,)), dma((np_,)), dma((np_,)), dma((np_,)),
            ],
            compiler_params=pltpu.CompilerParams(collective_id=0, has_side_effects=True, vmem_limit_bytes=60 * 1024 * 1024),
            name='moe',
        )(tokens, tab, w_gate, w_up, w_down)

    return jax.shard_map(device_step, mesh=mesh, in_specs=(row_spec, P(None, None), row_spec, expert_spec, expert_spec, expert_spec), out_specs=row_spec, check_vma=False)


def solution(mesh):
    return build(mesh, 4, ((0, 768), (768, 640), (1408, 640)))
```

time: 192 us -> 98.1 us (0.51)
  Pallas kernels: 0 us -> 94.6 us
  blocking collectives: 73.1 us -> 0 us
  waiting for transfers between devices: 54.8 us -> 0 us
  matrix products: 25.6 us -> 0 us
  local copies, waits for them, and re-layouts: 25.5 us -> 2.93 us
  other arithmetic: 6.8 us -> 0 us
  starting transfers between devices: 4.79 us -> 0 us
    pallas_call x0 -> x2, Pallas kernels: none -> 94.6 us  [the longest x1 92.5 us: device_step(): pl.pallas_call(functools.partial(moe_kernel, n, parts), out_shape=jax.Sha...]
    all_to_all x1 -> x0, blocking collectives: 73.1 us -> none  [device_step(): recv_rows = lax.all_to_all(send_rows, 'expert', 0, 0, tiled=True)]
    all_to_all x1 -> x0, waiting for transfers between devices: 54.8 us -> none  [device_step(): back_rows = lax.all_to_all(expert_out, 'expert', 0, 0, tiled=True)]
    dot_general x3 -> x0, matrix products: 25.6 us -> none  [the longest x1 14.6 us: device_step(): jnp.einsum('secf,efd->secd', hidden.astype(jnp.bfloat16), w_down, preferr...]
    gather x5 -> x0, local copies, waits for them, and re-layouts: 14.2 us -> none  [the longest x1 6.06 us: device_step(): jnp.take(back_rows.reshape(experts * capacity, width), slot_pos, axis=0)]
    convert_element_type x1 -> x0, local copies, waits for them, and re-layouts: 6.45 us -> none  [device_step(): jnp.einsum('secf,efd->secd', hidden.astype(jnp.bfloat16), w_down, preferr...]
    all_to_all x1 -> x0, starting transfers between devices: 4.79 us -> none  [device_step(): back_rows = lax.all_to_all(expert_out, 'expert', 0, 0, tiled=True)]
    reduce_sum x3 -> x0, other arithmetic: 3.68 us -> none  [the longest x1 3.32 us: device_step(): combined = jnp.sum(pair_rows * gate_vals[:, :, None], axis=1)]
  transfers between devices with their start and end apart: 1 -> 0, of which waited for: 1 -> 0; matrix products, arithmetic and copies ran while one was open for 2% -> 0% of each run, Pallas kernels for 0% -> 0%
where the time goes in v2:
time: 98.1 us; the launch traced here: 97.5 us
  Pallas kernels  94.6 us (96%)
  local copies, waits for them, and re-layouts  2.93 us (3%)
    pallas_call x1, Pallas kernels, device_step(): pl.pallas_call(functools.partial(moe_kernel, n, parts), out_shape=jax.Sha...  92.5 us
    unnamed x2, local copies, waits for them, and re-layouts  2.93 us
    pallas_call x1, Pallas kernels, device_step(): pl.pallas_call(prep_kernel, out_shape=jax.ShapeDtypeStruct((2 * CAP, expe...  2.05 us

profile of v2, /device:TPU:1, one launch (start us, length us, event | category | flops | bytes accessed | tf_op | source)
XLA Modules:
  0.0 97.5 jit_solution(13244232166206531333)
XLA Ops:
  0.0 1.4 %copy.7.r_ref = s32[32,8]{1,0:T(8,128)} copy(s32[32,8]{0,1:T(8,128)} %param.8) | data formatting | bytes 2048 | tf_op args[2]
  1.4 2.0 %prep.1.tab_ref = f32[16,128]{1,0:T(8,128)} custom-call(bf16[32,2048]{1,0:T(8,128)(2,1)} %x_ref.3, bf16[2048,128]{1,0:T(8,128)(2,1)} %wr_ref.1, s32[32,8]{1,0:T(8,128)} %copy.7.r_ref), custom_call_target="tpu_custom_call" | custom-call | tf_op jit(solution)/shard_map/prep/pallas_call | solution.py:245
  3.4 92.5 %moe.1 = bf16[32,2048]{1,0:T(8,128)(2,1)} custom-call(bf16[32,2048]{1,0:T(8,128)(2,1)} %x_ref.3, f32[16,128]{1,0:T(8,128)} %prep.1.tab_ref, bf16[1,2048,768]{2,1,0:T(8,128)(2,1)} %wg_hbm.1, bf16[1,2048,768]{2,1,0:T(8,128)(2,1)} %wu_hbm.1, bf16[1,768,2048]{2,1,0:T(8,128)(2,1)} %wd_hbm.1), custom_call_target="tpu_custom_call" | custom-call | tf_op jit(solution)/shard_map/moe/pallas_call | solution.py:251
  96.0 1.6 %copy.9 = bf16[32,2048]{1,0:T(8,128)(2,1)} copy(bf16[32,2048]{1,0:T(8,128)(2,1)} %moe.1) | data formatting | bytes 262144

commit v3 on v0

v3 whole, which is shorter than its diff:
```python
import functools

import jax
import jax.numpy as jnp
from jax import lax
from jax.experimental import pallas as pl
from jax.experimental.pallas import tpu as pltpu
from jax.sharding import PartitionSpec as P

F32 = jnp.float32
BF16 = jnp.bfloat16
CAP = 8


def _iota(shape, dim):
    return lax.broadcasted_iota(jnp.int32, shape, dim)


def _places(r):
    return (2 - r) % 3, (1 - r) % 3, (-r) % 3


def routing_table(x, wr, routes_t):
    tok, experts = x.shape[0], wr.shape[1]
    top_k = routes_t.shape[0]
    logits = jnp.dot(x, wr, preferred_element_type=F32)
    eye = (_iota((top_k, top_k), 0) == _iota((top_k, top_k), 1)).astype(BF16)
    routes = lax.dot_general(routes_t.astype(F32).astype(BF16), eye, (((0,), (0,)), ((), ())), preferred_element_type=F32)
    lane = _iota((tok, experts), 1).astype(F32)
    hit = jnp.zeros((tok, experts), F32)
    for j in range(top_k):
        hit += (routes[:, j:j + 1] == lane).astype(F32)
    on = hit > 0.5
    top = jnp.max(jnp.where(on, logits, -jnp.inf), axis=1, keepdims=True)
    e = jnp.where(on, jnp.exp(jnp.where(on, logits, top) - top), 0.0)
    gate = e / jnp.sum(e, axis=1, keepdims=True)
    below = (_iota((tok, tok), 1) < _iota((tok, tok), 0)).astype(BF16)
    rank = jnp.dot(below, hit.astype(BF16), preferred_element_type=F32)
    rank = jnp.where(on, rank, -1.0)
    row = _iota((tok, experts), 0).astype(F32)
    toks, gates = [], []
    for r in range(CAP):
        at = rank == r
        toks.append(jnp.sum(jnp.where(at, row + 1.0, 0.0), axis=0, keepdims=True) - 1.0)
        gates.append(jnp.sum(jnp.where(at, gate, 0.0), axis=0, keepdims=True))
    return jnp.concatenate(toks + gates, axis=0)


def moe_kernel(n, parts, x_ref, wr_ref, rt_ref, wg_hbm, wu_hbm, wd_hbm, y_ref, wg, wu, wd, rbuf, obuf, tab_ref, *rest):
    np_ = len(parts)
    tbuf, xbuf, sbuf, cbuf, bbuf, pbuf, abuf, mixbuf = [rest[i * np_:(i + 1) * np_] for i in range(8)]
    (w_sem, ta_s, ta_r, tb_s, tb_r, xa_s, xa_r, xb_s, xb_r, c_s, c_r, rc_s, rc_r, rb_s, rb_r, ra_s, ra_r) = rest[8 * np_:]
    tok, width = x_ref.shape
    experts = tab_ref.shape[1]
    me = lax.axis_index('expert')
    strides = (2 * n * n, 2 * n, 2)
    pos = tuple(lax.rem(me // s, n) for s in strides)
    core = lax.rem(me, 2)
    mod = lambda v: lax.rem(v, n)

    def order(p, cc):
        r0, r1 = _places(p % 3), _places((p + 1) % 3)
        return [(pos[i] + cc * (pos[j] - pos[i]), strides[i] + cc * (strides[j] - strides[i])) for i, j in zip(r0, r1)]

    mine = [order(p, core) for p in range(np_)]
    theirs = [order(p, 1 - core) for p in range(np_)]

    def moved(axis, d, flip=0):
        where, stride = axis
        other = me + (mod(where + d) - where) * stride
        return other + (1 - 2 * core) if flip else other

    def put(src, dst, send, recv, device):
        pltpu.make_async_remote_copy(src_ref=src, dst_ref=dst, send_sem=send, recv_sem=recv,
                                     device_id={'expert': device}, device_id_type=pl.DeviceIdType.MESH).start()

    def drain(ref, sem):
        pltpu.make_async_copy(ref, ref, sem).wait()

    def canon(p, cc, a, b, k):
        r0, r1 = _places(p % 3), _places((p + 1) % 3)
        v = (a, b, k)
        return [v[r0.index(j)] + cc * (v[r1.index(j)] - v[r0.index(j)]) for j in (0, 1)]

    loads = [pltpu.make_async_copy(src, dst, w_sem.at[i]) for i, (src, dst) in enumerate(((wg_hbm.at[0], wg), (wu_hbm.at[0], wu), (wd_hbm.at[0], wd)))]
    for load in loads:
        load.start()

    barrier = pltpu.get_barrier_semaphore()
    peers = [moved((pos[j], strides[j]), d, flip) for j in range(3) for d in range(1, n) for flip in (0, 1)] + [me + 1 - 2 * core]
    for peer in peers:
        pl.semaphore_signal(barrier, inc=1, device_id={'expert': peer}, device_id_type=pl.DeviceIdType.MESH)
    pl.semaphore_wait(barrier, len(peers))

    for axis, send, recv in ((0, xa_s, xa_r), (1, xb_s, xb_r)):
        for d in range(1, n):
            for p, (off, w) in enumerate(parts):
                (a, _), (b, _), _ = mine[p]
                put(x_ref.at[:, pl.ds(off, w)], xbuf[p].at[b, a], send.at[p], recv.at[p, d - 1], moved(mine[p][axis], d))
    tab_ref[...] = routing_table(x_ref[...], wr_ref[...], rt_ref[...])
    for p, (off, w) in enumerate(parts):
        (a, _), (b, _), _ = mine[p]
        xbuf[p][b, a] = x_ref[:, off:off + w]
        tbuf[p][b, a] = tab_ref[...]
    for p in range(np_):
        (a, _), (b, _), _ = mine[p]
        for d in range(1, n):
            put(tab_ref, tbuf[p].at[b, a], ta_s.at[p], ta_r.at[p], moved(mine[p][0], d))
    for da in range(1, n):
        for p in range(np_):
            (a, _), (b, _), _ = mine[p]
            src = mod(a + n - da)
            drain(xbuf[p].at[0, 0], xa_r.at[p, da - 1])
            for d in range(1, n):
                put(xbuf[p].at[b, src], xbuf[p].at[b, src], xb_s.at[p], xb_r.at[p, d - 1], moved(mine[p][1], d))
    for p in range(np_):
        b = mine[p][1][0]
        drain(tbuf[p].at[0, pl.ds(0, n - 1)], ta_r.at[p])
        for d in range(1, n):
            put(tbuf[p].at[b], tbuf[p].at[b], tb_s.at[p], tb_r.at[p], moved(mine[p][1], d))

    def select(p, db):
        off, w = parts[p]
        (a, _), (b, _), (k, _) = mine[p]
        bb = mod(b + n - db)
        table = tbuf[p][bb][:, :CAP].reshape(n * CAP, experts)
        shift = (_iota((n * CAP, 1), 0) // CAP * tok).astype(F32)
        lane = _iota((n * CAP, experts), 1)
        token = _iota((n * CAP, n * tok), 1).astype(F32)
        picks = []
        for q in range(2 * n):
            col = jnp.sum(jnp.where(lane == moved(mine[p][2], q // 2, q % 2), table, 0.0), axis=1, keepdims=True)
            want = jnp.where(col >= 0.0, col + shift, -1.0)
            picks.append((want == token).astype(F32))
        pick = jnp.concatenate(picks, axis=0).astype(BF16)
        rows = jnp.dot(pick, xbuf[p][bb].reshape(n * tok, w), preferred_element_type=F32).astype(BF16)
        sbuf[p][db] = rows.reshape(2 * n, n, CAP, w)

    def send_rows(p, db, i):
        off, w = parts[p]
        (a, _), (b, _), (k, _) = mine[p]
        bb = mod(b + n - db)
        aa = mod(i + 2 * n - bb - k)
        z, y = canon(p, core, aa, bb, k)
        for q in range(1, 2 * n):
            put(sbuf[p].at[db, q, aa], rbuf.at[i, z, y, core, :, pl.ds(off, w)], c_s.at[p], c_r.at[p, i], moved(mine[p][2], q // 2, q % 2))
        rbuf[i, z, y, core, :, off:off + w] = sbuf[p][db, 0, aa]

    def chunk_rows(i, dbs):
        for db in dbs:
            for p in range(np_):
                send_rows(p, db, i)

    def body(dbs):
        def run(i, carry):
            chunk_rows(i, dbs)
            return carry
        return run

    for p in range(np_):
        select(p, 0)
    lax.fori_loop(0, n, body((0,)), 0)
    for db in range(1, n):
        for p in range(np_):
            if db == 1:
                drain(tbuf[p].at[pl.ds(0, n - 1)], tb_r.at[p])
            drain(xbuf[p].at[0], xb_r.at[p, db - 1])
            select(p, db)
        chunk_rows(0, (db,))
    lax.fori_loop(1, n, body(tuple(range(1, n))), 0)

    cols = n * 2 * n * CAP
    for p in range(np_):
        (a, sa), (b, sb), (_, sc) = mine[p]
        slot = _iota((experts, cols), 1)
        ident = slot // (2 * n * CAP) * sb + lax.rem(slot // (2 * CAP), n) * sc + lax.rem(slot // CAP, 2) + a * sa
        spread = (ident == _iota((experts, cols), 0)).astype(BF16)
        keep = _iota((CAP, cols), 0) == lax.rem(_iota((CAP, cols), 1), CAP)
        for aa in range(n):
            tg = tbuf[p][b, aa]
            gate = tg[CAP:]
            g1 = gate.astype(BF16).astype(F32)
            g2 = (gate - g1).astype(BF16).astype(F32)
            g3 = gate - g1 - g2
            wide = jnp.dot(jnp.concatenate([tg[:CAP], g1, g2, g3], axis=0).astype(BF16), spread, preferred_element_type=F32)
            line = [jnp.sum(jnp.where(keep, wide[i * CAP:(i + 1) * CAP], 0.0), axis=0, keepdims=True) for i in range(4)]
            here = line[0] == _iota((tok, cols), 0).astype(F32)
            mixbuf[p][aa] = jnp.concatenate([jnp.where(here, line[i], 0.0) for i in (1, 2, 3)], axis=0).astype(BF16)

    for load in loads:
        load.wait()

    def expert(i, carry):
        for p in range(np_):
            drain(sbuf[p].at[:, pl.ds(0, 2 * n - 1), 0], c_r.at[p, i])
        rows = rbuf[i].reshape(n * n * 2 * CAP, width)
        g = jnp.dot(rows, wg[...], preferred_element_type=F32)
        u = jnp.dot(rows, wu[...], preferred_element_type=F32)
        h = (g * jax.nn.sigmoid(g) * u).astype(BF16)
        o = jnp.dot(h, wd[...], preferred_element_type=F32).astype(BF16)
        obuf[i] = o.reshape(n, n, 2, CAP, width)
        for db in list(range(1, n)) + [0]:
            for q in list(range(1, 2 * n)) + [0]:
                for p, (off, w) in enumerate(parts):
                    cc, axes = (1 - core, theirs[p]) if q % 2 else (core, mine[p])
                    (_, _), (b, _), (k, _) = axes
                    kk, bb = mod(k + q // 2), mod(b + db)
                    aa = mod(i + 2 * n - bb - kk)
                    z, y = canon(p, cc, aa, bb, kk)
                    if q:
                        put(obuf.at[i, z, y, cc, :, pl.ds(off, w)], cbuf[p].at[bb, aa, k * 2 + core],
                            rc_s.at[p], rc_r.at[p, db, i], moved(axes[2], q // 2, q % 2))
                    else:
                        cbuf[p][bb, aa, k * 2 + core] = obuf[i, z, y, cc, :, off:off + w]
        return carry

    lax.fori_loop(0, n, expert, 0)

    def forward(i):
        for db in list(range(1, n)) + [0]:
            for p in range(np_):
                _, (b, _), (k, _) = mine[p]
                bb = mod(b + db)
                aa = mod(i + 2 * n - bb - k)
                drain(cbuf[p].at[0, 0, pl.ds(0, 2 * n - 1)], rc_r.at[p, db, i])
                if db:
                    put(cbuf[p].at[bb, aa], bbuf[p].at[aa, b], rb_s.at[p], rb_r.at[p, i], moved(mine[p][1], db))
                else:
                    bbuf[p][aa, b] = cbuf[p][b, aa]

    def weigh(i):
        for p in range(np_):
            off, w = parts[p]
            (a, sa), (b, _), (k, _) = mine[p]
            aa = mod(i + 2 * n - b - k)
            drain(cbuf[p].at[0, pl.ds(0, n - 1)], rb_r.at[p, i])
            part = jnp.dot(mixbuf[p][aa], bbuf[p][aa].reshape(cols, w), preferred_element_type=F32)
            pbuf[p][i] = part[:tok] + part[tok:2 * tok] + part[2 * tok:]

            @pl.when(aa != a)
            def _():
                put(pbuf[p].at[i], abuf[p].at[a], ra_s.at[p], ra_r.at[p], me + (aa - a) * sa)

            @pl.when(aa == a)
            def _():
                abuf[p][a] = pbuf[p][i]

    for i in range(n):
        forward(i)
        if i:
            weigh(i - 1)
    weigh(n - 1)
    for p, (off, w) in enumerate(parts):
        drain(pbuf[p].at[pl.ds(0, n - 1)], ra_r.at[p])
        total = abuf[p][0]
        for i in range(1, n):
            total += abuf[p][i]
        y_ref[:, off:off + w] = total.astype(BF16)
    for p in range(np_):
        drain(tbuf[p].at[0, pl.ds(0, n - 1)], ta_s.at[p])
        drain(tbuf[p].at[pl.ds(0, n - 1)], tb_s.at[p])
        drain(xbuf[p].at[0, pl.ds(0, n - 1)], xa_s.at[p])
        drain(xbuf[p].at[pl.ds(0, n - 1)], xb_s.at[p])
        drain(sbuf[p].at[:, pl.ds(0, 2 * n - 1)], c_s.at[p])
        drain(cbuf[p].at[:, :, pl.ds(0, 2 * n - 1)], rc_s.at[p])
        drain(cbuf[p].at[pl.ds(0, n - 1)], rb_s.at[p])
        drain(pbuf[p].at[pl.ds(0, n - 1)], ra_s.at[p])


def build(mesh, n, parts):
    row_spec = P(('data', 'expert'), None)
    expert_spec = P('expert', None, None)
    vmem = pl.BlockSpec(memory_space=pltpu.VMEM)
    hbm = pl.BlockSpec(memory_space=pl.ANY)

    def device_step(tokens, w_router, routes, w_gate, w_up, w_down):
        tok, width = tokens.shape
        experts = w_router.shape[1]
        ff = w_gate.shape[2]
        dma = pltpu.SemaphoreType.DMA
        np_ = len(parts)
        cols = n * 2 * n * CAP
        return pl.pallas_call(
            functools.partial(moe_kernel, n, parts),
            out_shape=jax.ShapeDtypeStruct((tok, width), BF16),
            in_specs=[vmem, vmem, vmem, hbm, hbm, hbm], out_specs=vmem,
            scratch_shapes=[
                pltpu.VMEM((width, ff), BF16), pltpu.VMEM((width, ff), BF16), pltpu.VMEM((ff, width), BF16),
                pltpu.VMEM((n, n, n, 2, CAP, width), BF16), pltpu.VMEM((n, n, n, 2, CAP, width), BF16),
                pltpu.VMEM((2 * CAP, experts), F32),
                *[pltpu.VMEM((n, n, 2 * CAP, experts), F32) for _ in parts],
                *[pltpu.VMEM((n, n, tok, w), BF16) for _, w in parts],
                *[pltpu.VMEM((n, 2 * n, n, CAP, w), BF16) for _, w in parts],
                *[pltpu.VMEM((n, n, 2 * n, CAP, w), BF16) for _, w in parts],
                *[pltpu.VMEM((n, n, 2 * n, CAP, w), BF16) for _, w in parts],
                *[pltpu.VMEM((n, tok, w), F32) for _, w in parts],
                *[pltpu.VMEM((n, tok, w), F32) for _, w in parts],
                *[pltpu.VMEM((n, 3 * tok, cols), BF16) for _ in parts],
                dma((3,)), dma((np_,)), dma((np_,)), dma((np_,)), dma((np_,)),
                dma((np_,)), dma((np_, n - 1)), dma((np_,)), dma((np_, n - 1)), dma((np_,)), dma((np_, n)),
                dma((np_,)), dma((np_, n, n)), dma((np_,)), dma((np_, n)), dma((np_,)), dma((np_,)),
            ],
            compiler_params=pltpu.CompilerParams(collective_id=0, has_side_effects=True, vmem_limit_bytes=60 * 1024 * 1024),
            name='moe',
        )(tokens, w_router, routes.T, w_gate, w_up, w_down)

    return jax.shard_map(device_step, mesh=mesh, in_specs=(row_spec, P(None, None), row_spec, expert_spec, expert_spec, expert_spec), out_specs=row_spec, check_vma=False)


def solution(mesh):
    return build(mesh, 4, ((0, 768), (768, 640), (1408, 640)))
```

time: 192 us -> 79.9 us (0.42)
  Pallas kernels: 0 us -> 78.1 us
  blocking collectives: 73.1 us -> 0 us
  waiting for transfers between devices: 54.8 us -> 0 us
  matrix products: 25.6 us -> 0 us
  local copies, waits for them, and re-layouts: 25.5 us -> 1.57 us
  other arithmetic: 6.8 us -> 0 us
  starting transfers between devices: 4.79 us -> 0 us
    pallas_call x0 -> x1, Pallas kernels: none -> 78.1 us  [device_step(): pl.pallas_call(functools.partial(moe_kernel, n, parts), out_shape=jax.Sha...]
    all_to_all x1 -> x0, blocking collectives: 73.1 us -> none  [device_step(): recv_rows = lax.all_to_all(send_rows, 'expert', 0, 0, tiled=True)]
    all_to_all x1 -> x0, waiting for transfers between devices: 54.8 us -> none  [device_step(): back_rows = lax.all_to_all(expert_out, 'expert', 0, 0, tiled=True)]
    dot_general x3 -> x0, matrix products: 25.6 us -> none  [the longest x1 14.6 us: device_step(): jnp.einsum('secf,efd->secd', hidden.astype(jnp.bfloat16), w_down, preferr...]
    gather x5 -> x0, local copies, waits for them, and re-layouts: 14.2 us -> none  [the longest x1 6.06 us: device_step(): jnp.take(back_rows.reshape(experts * capacity, width), slot_pos, axis=0)]
    convert_element_type x1 -> x0, local copies, waits for them, and re-layouts: 6.45 us -> none  [device_step(): jnp.einsum('secf,efd->secd', hidden.astype(jnp.bfloat16), w_down, preferr...]
    all_to_all x1 -> x0, starting transfers between devices: 4.79 us -> none  [device_step(): back_rows = lax.all_to_all(expert_out, 'expert', 0, 0, tiled=True)]
    reduce_sum x3 -> x0, other arithmetic: 3.68 us -> none  [the longest x1 3.32 us: device_step(): combined = jnp.sum(pair_rows * gate_vals[:, :, None], axis=1)]
  transfers between devices with their start and end apart: 1 -> 0, of which waited for: 1 -> 0; matrix products, arithmetic and copies ran while one was open for 2% -> 0% of each run, Pallas kernels for 0% -> 0%
where the time goes in v3:
time: 79.9 us; the launch traced here: 79.7 us
  Pallas kernels  78.1 us (98%)
  local copies, waits for them, and re-layouts  1.57 us (2%)
    pallas_call x1, Pallas kernels, device_step(): pl.pallas_call(functools.partial(moe_kernel, n, parts), out_shape=jax.Sha...  78.1 us

profile of v3, /device:TPU:1, one launch (start us, length us, event | category | flops | bytes accessed | tf_op | source)
XLA Modules:
  0.0 79.7 jit_solution(11362792233294977907)
XLA Ops:
  0.0 78.1 %moe.1 = bf16[32,2048]{1,0:T(8,128)(2,1)} custom-call(bf16[32,2048]{1,0:T(8,128)(2,1)} %x_ref.1, bf16[2048,128]{1,0:T(8,128)(2,1)} %wr_ref.1, s32[8,32]{1,0:T(8,128)} %bitcast.1, bf16[1,2048,768]{2,1,0:T(8,128)(2,1)} %wg_hbm.1, bf16[1,2048,768]{2,1,0:T(8,128)(2,1)} %wu_hbm.1, bf16[1,768,2048]{2,1,0:T(8,128)(2,1)} %wd_hbm.1), custom_call_target="tpu_custom_call" | custom-call | tf_op jit(solution)/shard_map/moe/pallas_call | solution.py:283
  78.2 1.6 %copy.8 = bf16[32,2048]{1,0:T(8,128)(2,1)} copy(bf16[32,2048]{1,0:T(8,128)(2,1)} %moe.1) | data formatting | bytes 262144

commit v4 on v3

--- a/solution.py
+++ b/solution.py
@@ -46,10 +46,10 @@
     return jnp.concatenate(toks + gates, axis=0)
 
 
-def moe_kernel(n, parts, x_ref, wr_ref, rt_ref, wg_hbm, wu_hbm, wd_hbm, y_ref, wg, wu, wd, rbuf, obuf, tab_ref, *rest):
+def moe_kernel(n, parts, lefts, x_ref, wr_ref, rt_ref, wg_hbm, wu_hbm, wd_hbm, y_ref, wg, wu, wd, rbuf, obuf, tab_ref, *rest):
     np_ = len(parts)
-    tbuf, xbuf, sbuf, cbuf, bbuf, pbuf, abuf, mixbuf = [rest[i * np_:(i + 1) * np_] for i in range(8)]
-    (w_sem, ta_s, ta_r, tb_s, tb_r, xa_s, xa_r, xb_s, xb_r, c_s, c_r, rc_s, rc_r, rb_s, rb_r, ra_s, ra_r) = rest[8 * np_:]
+    tbuf, xbuf, sbuf, cbuf, farp, fari, nearp, neari, pbuf, abuf, mixbuf = [rest[i * np_:(i + 1) * np_] for i in range(11)]
+    (w_sem, ta_s, ta_r, tb_s, tb_r, xa_s, xa_r, xb_s, xb_r, c_s, c_r, rc_s, rc_r, rf_s, rf_r, rn_s, rn_r, ra_s, ra_r) = rest[11 * np_:]
     tok, width = x_ref.shape
     experts = tab_ref.shape[1]
     me = lax.axis_index('expert')
@@ -169,26 +169,30 @@
         chunk_rows(0, (db,))
     lax.fori_loop(1, n, body(tuple(range(1, n))), 0)
 
-    cols = n * 2 * n * CAP
+    cols = 2 * n * CAP
     for p in range(np_):
         (a, sa), (b, sb), (_, sc) = mine[p]
         slot = _iota((experts, cols), 1)
-        ident = slot // (2 * n * CAP) * sb + lax.rem(slot // (2 * CAP), n) * sc + lax.rem(slot // CAP, 2) + a * sa
+        ident = slot // (2 * CAP) * sc + lax.rem(slot // CAP, 2) + a * sa + b * sb
         spread = (ident == _iota((experts, cols), 0)).astype(BF16)
         keep = _iota((CAP, cols), 0) == lax.rem(_iota((CAP, cols), 1), CAP)
-        for aa in range(n):
-            tg = tbuf[p][b, aa]
-            gate = tg[CAP:]
+        for bb in range(n):
+            tg = tbuf[p][bb]
+            gate = tg[:, CAP:]
             g1 = gate.astype(BF16).astype(F32)
             g2 = (gate - g1).astype(BF16).astype(F32)
             g3 = gate - g1 - g2
-            wide = jnp.dot(jnp.concatenate([tg[:CAP], g1, g2, g3], axis=0).astype(BF16), spread, preferred_element_type=F32)
-            line = [jnp.sum(jnp.where(keep, wide[i * CAP:(i + 1) * CAP], 0.0), axis=0, keepdims=True) for i in range(4)]
-            here = line[0] == _iota((tok, cols), 0).astype(F32)
-            mixbuf[p][aa] = jnp.concatenate([jnp.where(here, line[i], 0.0) for i in (1, 2, 3)], axis=0).astype(BF16)
+            terms = jnp.concatenate([tg[:, :CAP], g1, g2, g3], axis=1).reshape(n * 4 * CAP, experts).astype(BF16)
+            wide = jnp.dot(terms, spread, preferred_element_type=F32)
+            for aa in range(n):
+                line = [jnp.sum(jnp.where(keep, wide[(aa * 4 + i) * CAP:(aa * 4 + i + 1) * CAP], 0.0), axis=0, keepdims=True) for i in range(4)]
+                here = line[0] == _iota((tok, cols), 0).astype(F32)
+                mixbuf[p][bb, aa] = jnp.concatenate([jnp.where(here, line[i], 0.0) for i in (1, 2, 3)], axis=0).astype(BF16)
 
     for load in loads:
         load.wait()
+
+    ring = (2, 1, 3, 0) if n == 4 else tuple(range(1, n)) + (0,)
 
     def expert(i, carry):
         for p in range(np_):
@@ -199,7 +203,7 @@
         h = (g * jax.nn.sigmoid(g) * u).astype(BF16)
         o = jnp.dot(h, wd[...], preferred_element_type=F32).astype(BF16)
         obuf[i] = o.reshape(n, n, 2, CAP, width)
-        for db in list(range(1, n)) + [0]:
+        for db in ring:
             for q in list(range(1, 2 * n)) + [0]:
                 for p, (off, w) in enumerate(parts):
                     cc, axes = (1 - core, theirs[p]) if q % 2 else (core, mine[p])
@@ -216,26 +220,41 @@
 
     lax.fori_loop(0, n, expert, 0)
 
-    def forward(i):
-        for db in list(range(1, n)) + [0]:
-            for p in range(np_):
-                _, (b, _), (k, _) = mine[p]
-                bb = mod(b + db)
-                aa = mod(i + 2 * n - bb - k)
-                drain(cbuf[p].at[0, 0, pl.ds(0, 2 * n - 1)], rc_r.at[p, db, i])
-                if db:
-                    put(cbuf[p].at[bb, aa], bbuf[p].at[aa, b], rb_s.at[p], rb_r.at[p, i], moved(mine[p][1], db))
-                else:
-                    bbuf[p][aa, b] = cbuf[p][b, aa]
-
-    def weigh(i):
-        for p in range(np_):
-            off, w = parts[p]
+    def line_sum(p, db, i):
+        w = parts[p][1]
+        _, (b, _), (k, _) = mine[p]
+        bb = mod(b + db)
+        aa = mod(i + 2 * n - bb - k)
+        drain(cbuf[p].at[0, 0, pl.ds(0, 2 * n - 1)], rc_r.at[p, db, i])
+        part = jnp.dot(mixbuf[p][bb, aa], cbuf[p][bb, aa].reshape(cols, w), preferred_element_type=F32)
+        return part[:tok] + part[tok:2 * tok] + part[2 * tok:]
+
+    def far(i):
+        for p in range(np_):
+            w, left = parts[p][1], lefts[p]
+            farp[p][i] = line_sum(p, 2, i)
+            put(farp[p].at[i, :, pl.ds(0, left)], fari[p].at[i, :, pl.ds(0, left)], rf_s.at[p], rf_r.at[p, i], moved(mine[p][1], 1))
+            put(farp[p].at[i, :, pl.ds(left, w - left)], fari[p].at[i, :, pl.ds(left, w - left)], rf_s.at[p], rf_r.at[p, i], moved(mine[p][1], n - 1))
+
+    def near(i):
+        for p in range(np_):
+            left = lefts[p]
+            up, down = line_sum(p, 1, i), line_sum(p, n - 1, i)
+            drain(fari[p].at[i], rf_r.at[p, i])
+            nearp[p][i, 0, :, :left] = up[:, :left] + fari[p][i, :, :left]
+            nearp[p][i, 0, :, left:] = up[:, left:]
+            put(nearp[p].at[i, 0], neari[p].at[i, 0], rn_s.at[p], rn_r.at[p, i], moved(mine[p][1], 1))
+            nearp[p][i, 1, :, :left] = down[:, :left]
+            nearp[p][i, 1, :, left:] = down[:, left:] + fari[p][i, :, left:]
+            put(nearp[p].at[i, 1], neari[p].at[i, 1], rn_s.at[p], rn_r.at[p, i], moved(mine[p][1], n - 1))
+
+    def here(i):
+        for p in range(np_):
             (a, sa), (b, _), (k, _) = mine[p]
             aa = mod(i + 2 * n - b - k)
-            drain(cbuf[p].at[0, pl.ds(0, n - 1)], rb_r.at[p, i])
-            part = jnp.dot(mixbuf[p][aa], bbuf[p][aa].reshape(cols, w), preferred_element_type=F32)
-            pbuf[p][i] = part[:tok] + part[tok:2 * tok] + part[2 * tok:]
+            own = line_sum(p, 0, i)
+            drain(neari[p].at[i], rn_r.at[p, i])
+            pbuf[p][i] = own + neari[p][i, 0] + neari[p][i, 1]
 
             @pl.when(aa != a)
             def _():
@@ -245,11 +264,13 @@
             def _():
                 abuf[p][a] = pbuf[p][i]
 
-    for i in range(n):
-        forward(i)
-        if i:
-            weigh(i - 1)
-    weigh(n - 1)
+    for t in range(n + 2):
+        if t < n:
+            far(t)
+        if 0 <= t - 1 < n:
+            near(t - 1)
+        if t >= 2:
+            here(t - 2)
     for p, (off, w) in enumerate(parts):
         drain(pbuf[p].at[pl.ds(0, n - 1)], ra_r.at[p])
         total = abuf[p][0]
@@ -263,11 +284,12 @@
         drain(xbuf[p].at[pl.ds(0, n - 1)], xb_s.at[p])
         drain(sbuf[p].at[:, pl.ds(0, 2 * n - 1)], c_s.at[p])
         drain(cbuf[p].at[:, :, pl.ds(0, 2 * n - 1)], rc_s.at[p])
-        drain(cbuf[p].at[pl.ds(0, n - 1)], rb_s.at[p])
+        drain(farp[p], rf_s.at[p])
+        drain(nearp[p], rn_s.at[p])
         drain(pbuf[p].at[pl.ds(0, n - 1)], ra_s.at[p])
 
 
-def build(mesh, n, parts):
+def build(mesh, n, parts, lefts):
     row_spec = P(('data', 'expert'), None)
     expert_spec = P('expert', None, None)
     vmem = pl.BlockSpec(memory_space=pltpu.VMEM)
@@ -279,9 +301,9 @@
         ff = w_gate.shape[2]
         dma = pltpu.SemaphoreType.DMA
         np_ = len(parts)
-        cols = n * 2 * n * CAP
+        cols = 2 * n * CAP
         return pl.pallas_call(
-            functools.partial(moe_kernel, n, parts),
+            functools.partial(moe_kernel, n, parts, lefts),
             out_shape=jax.ShapeDtypeStruct((tok, width), BF16),
             in_specs=[vmem, vmem, vmem, hbm, hbm, hbm], out_specs=vmem,
             scratch_shapes=[
@@ -292,13 +314,16 @@
                 *[pltpu.VMEM((n, n, tok, w), BF16) for _, w in parts],
                 *[pltpu.VMEM((n, 2 * n, n, CAP, w), BF16) for _, w in parts],
                 *[pltpu.VMEM((n, n, 2 * n, CAP, w), BF16) for _, w in parts],
-                *[pltpu.VMEM((n, n, 2 * n, CAP, w), BF16) for _, w in parts],
                 *[pltpu.VMEM((n, tok, w), F32) for _, w in parts],
                 *[pltpu.VMEM((n, tok, w), F32) for _, w in parts],
-                *[pltpu.VMEM((n, 3 * tok, cols), BF16) for _ in parts],
+                *[pltpu.VMEM((n, 2, tok, w), F32) for _, w in parts],
+                *[pltpu.VMEM((n, 2, tok, w), F32) for _, w in parts],
+                *[pltpu.VMEM((n, tok, w), F32) for _, w in parts],
+                *[pltpu.VMEM((n, tok, w), F32) for _, w in parts],
+                *[pltpu.VMEM((n, n, 3 * tok, cols), BF16) for _ in parts],
                 dma((3,)), dma((np_,)), dma((np_,)), dma((np_,)), dma((np_,)),
                 dma((np_,)), dma((np_, n - 1)), dma((np_,)), dma((np_, n - 1)), dma((np_,)), dma((np_, n)),
-                dma((np_,)), dma((np_, n, n)), dma((np_,)), dma((np_, n)), dma((np_,)), dma((np_,)),
+                dma((np_,)), dma((np_, n, n)), dma((np_,)), dma((np_, n)), dma((np_,)), dma((np_, n)), dma((np_,)), dma((np_,)),
             ],
             compiler_params=pltpu.CompilerParams(collective_id=0, has_side_effects=True, vmem_limit_bytes=60 * 1024 * 1024),
             name='moe',
@@ -308,4 +333,4 @@
 
 
 def solution(mesh):
-    return build(mesh, 4, ((0, 768), (768, 640), (1408, 640)))
+    return build(mesh, 4, ((0, 768), (768, 640), (1408, 640)), (384, 384, 256))

time: 79.9 us -> 77.7 us (0.972)
  the two profiles are of different devices: /device:TPU:1 before, /device:TPU:6 now
where the time goes in v4:
time: 77.7 us; the launch traced here: 77.5 us
  Pallas kernels  76 us (98%)
  local copies, waits for them, and re-layouts  1.57 us (2%)
    pallas_call x1, Pallas kernels, device_step(): pl.pallas_call(functools.partial(moe_kernel, n, parts, lefts), out_shape=...  76 us
    unnamed x1, local copies, waits for them, and re-layouts  1.57 us

profile of v4, /device:TPU:6, one launch (start us, length us, event | category | flops | bytes accessed | tf_op | source)
XLA Modules:
  0.0 77.5 jit_solution(17976132189307619555)
XLA Ops:
  0.0 76.0 %moe.1 = bf16[32,2048]{1,0:T(8,128)(2,1)} custom-call(bf16[32,2048]{1,0:T(8,128)(2,1)} %x_ref.1, bf16[2048,128]{1,0:T(8,128)(2,1)} %wr_ref.1, s32[8,32]{1,0:T(8,128)} %bitcast.1, bf16[1,2048,768]{2,1,0:T(8,128)(2,1)} %wg_hbm.1, bf16[1,2048,768]{2,1,0:T(8,128)(2,1)} %wu_hbm.1, bf16[1,768,2048]{2,1,0:T(8,128)(2,1)} %wd_hbm.1), custom_call_target="tpu_custom_call" | custom-call | tf_op jit(solution)/shard_map/moe/pallas_call | solution.py:305
  76.0 1.6 %copy.8 = bf16[32,2048]{1,0:T(8,128)(2,1)} copy(bf16[32,2048]{1,0:T(8,128)(2,1)} %moe.1) | data formatting | bytes 262144

commit v5 on v4

--- a/solution.py
+++ b/solution.py
@@ -46,10 +46,10 @@
     return jnp.concatenate(toks + gates, axis=0)
 
 
-def moe_kernel(n, parts, lefts, x_ref, wr_ref, rt_ref, wg_hbm, wu_hbm, wd_hbm, y_ref, wg, wu, wd, rbuf, obuf, tab_ref, *rest):
+def moe_kernel(n, parts, lefts, x_hbm, wr_hbm, rt_hbm, wg_hbm, wu_hbm, wd_hbm, y_ref, x_ref, wr_ref, rt_ref, wg, wu, wd, rbuf, obuf, tab_ref, *rest):
     np_ = len(parts)
     tbuf, xbuf, sbuf, cbuf, farp, fari, nearp, neari, pbuf, abuf, mixbuf = [rest[i * np_:(i + 1) * np_] for i in range(11)]
-    (w_sem, ta_s, ta_r, tb_s, tb_r, xa_s, xa_r, xb_s, xb_r, c_s, c_r, rc_s, rc_r, rf_s, rf_r, rn_s, rn_r, ra_s, ra_r) = rest[11 * np_:]
+    (w_sem, ta_s, ta_r, tb_s, tb_r, xa_s, xa_r, xb_s, xb_r, xd_s, xd_r, c_s, c_r, rc_s, rc_r, rf_s, rf_r, rn_s, rn_r, ra_s, ra_r) = rest[11 * np_:]
     tok, width = x_ref.shape
     experts = tab_ref.shape[1]
     me = lax.axis_index('expert')
@@ -82,7 +82,7 @@
         v = (a, b, k)
         return [v[r0.index(j)] + cc * (v[r1.index(j)] - v[r0.index(j)]) for j in (0, 1)]
 
-    loads = [pltpu.make_async_copy(src, dst, w_sem.at[i]) for i, (src, dst) in enumerate(((wg_hbm.at[0], wg), (wu_hbm.at[0], wu), (wd_hbm.at[0], wd)))]
+    loads = [pltpu.make_async_copy(src, dst, w_sem.at[i]) for i, (src, dst) in enumerate(((x_hbm, x_ref), (wr_hbm, wr_ref), (rt_hbm, rt_ref), (wg_hbm.at[0], wg), (wu_hbm.at[0], wu), (wd_hbm.at[0], wd)))]
     for load in loads:
         load.start()
 
@@ -90,34 +90,58 @@
     peers = [moved((pos[j], strides[j]), d, flip) for j in range(3) for d in range(1, n) for flip in (0, 1)] + [me + 1 - 2 * core]
     for peer in peers:
         pl.semaphore_signal(barrier, inc=1, device_id={'expert': peer}, device_id_type=pl.DeviceIdType.MESH)
+    for load in loads[:3]:
+        load.wait()
     pl.semaphore_wait(barrier, len(peers))
 
-    for axis, send, recv in ((0, xa_s, xa_r), (1, xb_s, xb_r)):
-        for d in range(1, n):
-            for p, (off, w) in enumerate(parts):
-                (a, _), (b, _), _ = mine[p]
-                put(x_ref.at[:, pl.ds(off, w)], xbuf[p].at[b, a], send.at[p], recv.at[p, d - 1], moved(mine[p][axis], d))
+    near_first, far_first = (1, 3, 2), (2, 1, 3)
+
+    for d in far_first:
+        for p, (off, w) in enumerate(parts):
+            (a, _), (b, _), _ = mine[p]
+            put(x_ref.at[:, pl.ds(off, w)], xbuf[p].at[b, a], xa_s.at[p], xa_r.at[p, d - 1], moved(mine[p][0], d))
+    for side in (0, 1):
+        for p, (off, w) in enumerate(parts):
+            (a, _), (b, _), _ = mine[p]
+            put(x_ref.at[:, pl.ds(off, w)], xbuf[p].at[b, a], xb_s.at[p], xb_r.at[p, side, 0], moved(mine[p][1], 1 + 2 * side))
     tab_ref[...] = routing_table(x_ref[...], wr_ref[...], rt_ref[...])
     for p, (off, w) in enumerate(parts):
         (a, _), (b, _), _ = mine[p]
         xbuf[p][b, a] = x_ref[:, off:off + w]
         tbuf[p][b, a] = tab_ref[...]
-    for p in range(np_):
-        (a, _), (b, _), _ = mine[p]
-        for d in range(1, n):
+    for d in far_first:
+        for p in range(np_):
+            (a, _), (b, _), _ = mine[p]
             put(tab_ref, tbuf[p].at[b, a], ta_s.at[p], ta_r.at[p], moved(mine[p][0], d))
-    for da in range(1, n):
+
+    def along_b(da):
         for p in range(np_):
             (a, _), (b, _), _ = mine[p]
             src = mod(a + n - da)
             drain(xbuf[p].at[0, 0], xa_r.at[p, da - 1])
-            for d in range(1, n):
-                put(xbuf[p].at[b, src], xbuf[p].at[b, src], xb_s.at[p], xb_r.at[p, d - 1], moved(mine[p][1], d))
+            for side in (0, 1):
+                put(xbuf[p].at[b, src], xbuf[p].at[b, src], xb_s.at[p], xb_r.at[p, side, da], moved(mine[p][1], 1 + 2 * side))
+
+    def onward(da):
+        for side in (0, 1):
+            for p, (off, w) in enumerate(parts):
+                (a, _), (b, _), _ = mine[p]
+                src, bb = mod(a + n - da), mod(b + n - 1 - 2 * side)
+                drain(xbuf[p].at[0, 0], xb_r.at[p, side, da])
+                half = pl.ds(lefts[p], w - lefts[p]) if side else pl.ds(0, lefts[p])
+                put(xbuf[p].at[bb, src, :, half], xbuf[p].at[bb, src, :, half], xd_s.at[p], xd_r.at[p], moved(mine[p][1], 1 + 2 * side))
+
+    along_b(1)
+    along_b(3)
+    onward(0)
+    along_b(2)
     for p in range(np_):
         b = mine[p][1][0]
         drain(tbuf[p].at[0, pl.ds(0, n - 1)], ta_r.at[p])
-        for d in range(1, n):
+        for d in far_first:
             put(tbuf[p].at[b], tbuf[p].at[b], tb_s.at[p], tb_r.at[p], moved(mine[p][1], d))
+
+    q_order = (4, 5, 2, 3, 6, 7, 1)
 
     def select(p, db):
         off, w = parts[p]
@@ -142,7 +166,7 @@
         bb = mod(b + n - db)
         aa = mod(i + 2 * n - bb - k)
         z, y = canon(p, core, aa, bb, k)
-        for q in range(1, 2 * n):
+        for q in q_order:
             put(sbuf[p].at[db, q, aa], rbuf.at[i, z, y, core, :, pl.ds(off, w)], c_s.at[p], c_r.at[p, i], moved(mine[p][2], q // 2, q % 2))
         rbuf[i, z, y, core, :, off:off + w] = sbuf[p][db, 0, aa]
 
@@ -160,14 +184,21 @@
     for p in range(np_):
         select(p, 0)
     lax.fori_loop(0, n, body((0,)), 0)
-    for db in range(1, n):
-        for p in range(np_):
-            if db == 1:
-                drain(tbuf[p].at[pl.ds(0, n - 1)], tb_r.at[p])
-            drain(xbuf[p].at[0], xb_r.at[p, db - 1])
+    for da in near_first:
+        onward(da)
+    for p in range(np_):
+        drain(tbuf[p].at[pl.ds(0, n - 1)], tb_r.at[p])
+    for db in (1, 3):
+        for p in range(np_):
             select(p, db)
         chunk_rows(0, (db,))
-    lax.fori_loop(1, n, body(tuple(range(1, n))), 0)
+    chunk_rows(1, (1, 3))
+    for p in range(np_):
+        drain(xbuf[p].at[0], xd_r.at[p])
+        select(p, 2)
+    chunk_rows(0, (2,))
+    chunk_rows(1, (2,))
+    lax.fori_loop(2, n, body((1, 3, 2)), 0)
 
     cols = 2 * n * CAP
     for p in range(np_):
@@ -189,7 +220,7 @@
                 here = line[0] == _iota((tok, cols), 0).astype(F32)
                 mixbuf[p][bb, aa] = jnp.concatenate([jnp.where(here, line[i], 0.0) for i in (1, 2, 3)], axis=0).astype(BF16)
 
-    for load in loads:
+    for load in loads[3:]:
         load.wait()
 
     ring = (2, 1, 3, 0) if n == 4 else tuple(range(1, n)) + (0,)
@@ -204,7 +235,7 @@
         o = jnp.dot(h, wd[...], preferred_element_type=F32).astype(BF16)
         obuf[i] = o.reshape(n, n, 2, CAP, width)
         for db in ring:
-            for q in list(range(1, 2 * n)) + [0]:
+            for q in q_order + (0,):
                 for p, (off, w) in enumerate(parts):
                     cc, axes = (1 - core, theirs[p]) if q % 2 else (core, mine[p])
                     (_, _), (b, _), (k, _) = axes
@@ -281,7 +312,8 @@
         drain(tbuf[p].at[0, pl.ds(0, n - 1)], ta_s.at[p])
         drain(tbuf[p].at[pl.ds(0, n - 1)], tb_s.at[p])
         drain(xbuf[p].at[0, pl.ds(0, n - 1)], xa_s.at[p])
-        drain(xbuf[p].at[pl.ds(0, n - 1)], xb_s.at[p])
+        drain(xbuf[p].at[pl.ds(0, 2)], xb_s.at[p])
+        drain(xbuf[p].at[0], xd_s.at[p])
         drain(sbuf[p].at[:, pl.ds(0, 2 * n - 1)], c_s.at[p])
         drain(cbuf[p].at[:, :, pl.ds(0, 2 * n - 1)], rc_s.at[p])
         drain(farp[p], rf_s.at[p])
@@ -305,8 +337,9 @@
         return pl.pallas_call(
             functools.partial(moe_kernel, n, parts, lefts),
             out_shape=jax.ShapeDtypeStruct((tok, width), BF16),
-            in_specs=[vmem, vmem, vmem, hbm, hbm, hbm], out_specs=vmem,
+            in_specs=[hbm] * 6, out_specs=vmem,
             scratch_shapes=[
+                pltpu.VMEM((tok, width), BF16), pltpu.VMEM((width, experts), BF16), pltpu.VMEM((routes.shape[1], tok), jnp.int32),
                 pltpu.VMEM((width, ff), BF16), pltpu.VMEM((width, ff), BF16), pltpu.VMEM((ff, width), BF16),
                 pltpu.VMEM((n, n, n, 2, CAP, width), BF16), pltpu.VMEM((n, n, n, 2, CAP, width), BF16),
                 pltpu.VMEM((2 * CAP, experts), F32),
@@ -321,8 +354,8 @@
                 *[pltpu.VMEM((n, tok, w), F32) for _, w in parts],
                 *[pltpu.VMEM((n, tok, w), F32) for _, w in parts],
                 *[pltpu.VMEM((n, n, 3 * tok, cols), BF16) for _ in parts],
-                dma((3,)), dma((np_,)), dma((np_,)), dma((np_,)), dma((np_,)),
-                dma((np_,)), dma((np_, n - 1)), dma((np_,)), dma((np_, n - 1)), dma((np_,)), dma((np_, n)),
+                dma((6,)), dma((np_,)), dma((np_,)), dma((np_,)), dma((np_,)),
+                dma((np_,)), dma((np_, n - 1)), dma((np_,)), dma((np_, 2, n)), dma((np_,)), dma((np_,)), dma((np_,)), dma((np_, n)),
                 dma((np_,)), dma((np_, n, n)), dma((np_,)), dma((np_, n)), dma((np_,)), dma((np_, n)), dma((np_,)), dma((np_,)),
             ],
             compiler_params=pltpu.CompilerParams(collective_id=0, has_side_effects=True, vmem_limit_bytes=60 * 1024 * 1024),

time: 77.7 us -> 78 us (level)
  the two profiles are of different devices: /device:TPU:6 before, /device:TPU:1 now
where the time goes in v5:
time: 78 us; the launch traced here: 77.8 us
  Pallas kernels  76.2 us (98%)
  local copies, waits for them, and re-layouts  1.57 us (2%)
    pallas_call x1, Pallas kernels, device_step(): pl.pallas_call(functools.partial(moe_kernel, n, parts, lefts), out_shape=...  76.2 us
    unnamed x1, local copies, waits for them, and re-layouts  1.57 us

profile of v5, /device:TPU:1, one launch (start us, length us, event | category | flops | bytes accessed | tf_op | source)
XLA Modules:
  0.0 77.8 jit_solution(11646260788064250604)
XLA Ops:
  0.0 76.2 %moe.1 = bf16[32,2048]{1,0:T(8,128)(2,1)} custom-call(bf16[32,2048]{1,0:T(8,128)(2,1)} %x_hbm.1, bf16[2048,128]{1,0:T(8,128)(2,1)} %wr_hbm.1, s32[8,32]{1,0:T(8,128)} %bitcast.1, bf16[1,2048,768]{2,1,0:T(8,128)(2,1)} %wg_hbm.1, bf16[1,2048,768]{2,1,0:T(8,128)(2,1)} %wu_hbm.1, bf16[1,768,2048]{2,1,0:T(8,128)(2,1)} %wd_hbm.1), custom_call_target="tpu_custom_call" | custom-call | tf_op jit(solution)/shard_map/moe/pallas_call | solution.py:337
  76.2 1.6 %copy.8 = bf16[32,2048]{1,0:T(8,128)(2,1)} copy(bf16[32,2048]{1,0:T(8,128)(2,1)} %moe.1) | data formatting | bytes 262144

commit v6 on v4

--- a/solution.py
+++ b/solution.py
@@ -46,7 +46,7 @@
     return jnp.concatenate(toks + gates, axis=0)
 
 
-def moe_kernel(n, parts, lefts, x_ref, wr_ref, rt_ref, wg_hbm, wu_hbm, wd_hbm, y_ref, wg, wu, wd, rbuf, obuf, tab_ref, *rest):
+def moe_kernel(n, parts, lefts, x_hbm, wr_hbm, rt_hbm, wg_hbm, wu_hbm, wd_hbm, y_ref, x_ref, wr_ref, rt_ref, wg, wu, wd, rbuf, obuf, tab_ref, *rest):
     np_ = len(parts)
     tbuf, xbuf, sbuf, cbuf, farp, fari, nearp, neari, pbuf, abuf, mixbuf = [rest[i * np_:(i + 1) * np_] for i in range(11)]
     (w_sem, ta_s, ta_r, tb_s, tb_r, xa_s, xa_r, xb_s, xb_r, c_s, c_r, rc_s, rc_r, rf_s, rf_r, rn_s, rn_r, ra_s, ra_r) = rest[11 * np_:]
@@ -82,7 +82,7 @@
         v = (a, b, k)
         return [v[r0.index(j)] + cc * (v[r1.index(j)] - v[r0.index(j)]) for j in (0, 1)]
 
-    loads = [pltpu.make_async_copy(src, dst, w_sem.at[i]) for i, (src, dst) in enumerate(((wg_hbm.at[0], wg), (wu_hbm.at[0], wu), (wd_hbm.at[0], wd)))]
+    loads = [pltpu.make_async_copy(src, dst, w_sem.at[i]) for i, (src, dst) in enumerate(((x_hbm, x_ref), (wr_hbm, wr_ref), (rt_hbm, rt_ref), (wg_hbm.at[0], wg), (wu_hbm.at[0], wu), (wd_hbm.at[0], wd)))]
     for load in loads:
         load.start()
 
@@ -90,10 +90,14 @@
     peers = [moved((pos[j], strides[j]), d, flip) for j in range(3) for d in range(1, n) for flip in (0, 1)] + [me + 1 - 2 * core]
     for peer in peers:
         pl.semaphore_signal(barrier, inc=1, device_id={'expert': peer}, device_id_type=pl.DeviceIdType.MESH)
+    for load in loads[:3]:
+        load.wait()
     pl.semaphore_wait(barrier, len(peers))
 
+    near_first, far_first = (1, 3, 2), (2, 1, 3)
+
     for axis, send, recv in ((0, xa_s, xa_r), (1, xb_s, xb_r)):
-        for d in range(1, n):
+        for d in far_first:
             for p, (off, w) in enumerate(parts):
                 (a, _), (b, _), _ = mine[p]
                 put(x_ref.at[:, pl.ds(off, w)], xbuf[p].at[b, a], send.at[p], recv.at[p, d - 1], moved(mine[p][axis], d))
@@ -102,22 +106,24 @@
         (a, _), (b, _), _ = mine[p]
         xbuf[p][b, a] = x_ref[:, off:off + w]
         tbuf[p][b, a] = tab_ref[...]
-    for p in range(np_):
-        (a, _), (b, _), _ = mine[p]
-        for d in range(1, n):
+    for d in far_first:
+        for p in range(np_):
+            (a, _), (b, _), _ = mine[p]
             put(tab_ref, tbuf[p].at[b, a], ta_s.at[p], ta_r.at[p], moved(mine[p][0], d))
-    for da in range(1, n):
+    for da in near_first:
         for p in range(np_):
             (a, _), (b, _), _ = mine[p]
             src = mod(a + n - da)
             drain(xbuf[p].at[0, 0], xa_r.at[p, da - 1])
-            for d in range(1, n):
+            for d in far_first:
                 put(xbuf[p].at[b, src], xbuf[p].at[b, src], xb_s.at[p], xb_r.at[p, d - 1], moved(mine[p][1], d))
     for p in range(np_):
         b = mine[p][1][0]
         drain(tbuf[p].at[0, pl.ds(0, n - 1)], ta_r.at[p])
-        for d in range(1, n):
+        for d in far_first:
             put(tbuf[p].at[b], tbuf[p].at[b], tb_s.at[p], tb_r.at[p], moved(mine[p][1], d))
+
+    q_order = (4, 5, 2, 3, 6, 7, 1)
 
     def select(p, db):
         off, w = parts[p]
@@ -142,7 +148,7 @@
         bb = mod(b + n - db)
         aa = mod(i + 2 * n - bb - k)
         z, y = canon(p, core, aa, bb, k)
-        for q in range(1, 2 * n):
+        for q in q_order:
             put(sbuf[p].at[db, q, aa], rbuf.at[i, z, y, core, :, pl.ds(off, w)], c_s.at[p], c_r.at[p, i], moved(mine[p][2], q // 2, q % 2))
         rbuf[i, z, y, core, :, off:off + w] = sbuf[p][db, 0, aa]
 
@@ -160,14 +166,14 @@
     for p in range(np_):
         select(p, 0)
     lax.fori_loop(0, n, body((0,)), 0)
-    for db in range(1, n):
-        for p in range(np_):
-            if db == 1:
-                drain(tbuf[p].at[pl.ds(0, n - 1)], tb_r.at[p])
+    for p in range(np_):
+        drain(tbuf[p].at[pl.ds(0, n - 1)], tb_r.at[p])
+    for db in near_first:
+        for p in range(np_):
             drain(xbuf[p].at[0], xb_r.at[p, db - 1])
             select(p, db)
         chunk_rows(0, (db,))
-    lax.fori_loop(1, n, body(tuple(range(1, n))), 0)
+    lax.fori_loop(1, n, body(near_first), 0)
 
     cols = 2 * n * CAP
     for p in range(np_):
@@ -189,7 +195,7 @@
                 here = line[0] == _iota((tok, cols), 0).astype(F32)
                 mixbuf[p][bb, aa] = jnp.concatenate([jnp.where(here, line[i], 0.0) for i in (1, 2, 3)], axis=0).astype(BF16)
 
-    for load in loads:
+    for load in loads[3:]:
         load.wait()
 
     ring = (2, 1, 3, 0) if n == 4 else tuple(range(1, n)) + (0,)
@@ -204,7 +210,7 @@
         o = jnp.dot(h, wd[...], preferred_element_type=F32).astype(BF16)
         obuf[i] = o.reshape(n, n, 2, CAP, width)
         for db in ring:
-            for q in list(range(1, 2 * n)) + [0]:
+            for q in q_order + (0,):
                 for p, (off, w) in enumerate(parts):
                     cc, axes = (1 - core, theirs[p]) if q % 2 else (core, mine[p])
                     (_, _), (b, _), (k, _) = axes
@@ -231,14 +237,14 @@
 
     def far(i):
         for p in range(np_):
-            w, left = parts[p][1], lefts[p]
+            w, left = parts[p][1], lefts[i % 2][p]
             farp[p][i] = line_sum(p, 2, i)
             put(farp[p].at[i, :, pl.ds(0, left)], fari[p].at[i, :, pl.ds(0, left)], rf_s.at[p], rf_r.at[p, i], moved(mine[p][1], 1))
             put(farp[p].at[i, :, pl.ds(left, w - left)], fari[p].at[i, :, pl.ds(left, w - left)], rf_s.at[p], rf_r.at[p, i], moved(mine[p][1], n - 1))
 
     def near(i):
         for p in range(np_):
-            left = lefts[p]
+            left = lefts[i % 2][p]
             up, down = line_sum(p, 1, i), line_sum(p, n - 1, i)
             drain(fari[p].at[i], rf_r.at[p, i])
             nearp[p][i, 0, :, :left] = up[:, :left] + fari[p][i, :, :left]
@@ -293,7 +299,7 @@
     row_spec = P(('data', 'expert'), None)
     expert_spec = P('expert', None, None)
     vmem = pl.BlockSpec(memory_space=pltpu.VMEM)
-    hbm = pl.BlockSpec(memory_space=pl.ANY)
+    hbm = pl.BlockSpec(memory_space=pltpu.HBM)
 
     def device_step(tokens, w_router, routes, w_gate, w_up, w_down):
         tok, width = tokens.shape
@@ -304,9 +310,10 @@
         cols = 2 * n * CAP
         return pl.pallas_call(
             functools.partial(moe_kernel, n, parts, lefts),
-            out_shape=jax.ShapeDtypeStruct((tok, width), BF16),
-            in_specs=[vmem, vmem, vmem, hbm, hbm, hbm], out_specs=vmem,
+            out_shape=pltpu.VMEM((tok, width), BF16),
+            in_specs=[hbm] * 6, out_specs=vmem,
             scratch_shapes=[
+                pltpu.VMEM((tok, width), BF16), pltpu.VMEM((width, experts), BF16), pltpu.VMEM((routes.shape[1], tok), jnp.int32),
                 pltpu.VMEM((width, ff), BF16), pltpu.VMEM((width, ff), BF16), pltpu.VMEM((ff, width), BF16),
                 pltpu.VMEM((n, n, n, 2, CAP, width), BF16), pltpu.VMEM((n, n, n, 2, CAP, width), BF16),
                 pltpu.VMEM((2 * CAP, experts), F32),
@@ -321,11 +328,11 @@
                 *[pltpu.VMEM((n, tok, w), F32) for _, w in parts],
                 *[pltpu.VMEM((n, tok, w), F32) for _, w in parts],
                 *[pltpu.VMEM((n, n, 3 * tok, cols), BF16) for _ in parts],
-                dma((3,)), dma((np_,)), dma((np_,)), dma((np_,)), dma((np_,)),
+                dma((6,)), dma((np_,)), dma((np_,)), dma((np_,)), dma((np_,)),
                 dma((np_,)), dma((np_, n - 1)), dma((np_,)), dma((np_, n - 1)), dma((np_,)), dma((np_, n)),
                 dma((np_,)), dma((np_, n, n)), dma((np_,)), dma((np_, n)), dma((np_,)), dma((np_, n)), dma((np_,)), dma((np_,)),
             ],
-            compiler_params=pltpu.CompilerParams(collective_id=0, has_side_effects=True, vmem_limit_bytes=60 * 1024 * 1024),
+            compiler_params=pltpu.CompilerParams(collective_id=0, has_side_effects=True, vmem_limit_bytes=57 * 1024 * 1024),
             name='moe',
         )(tokens, w_router, routes.T, w_gate, w_up, w_down)
 
@@ -333,4 +340,4 @@
 
 
 def solution(mesh):
-    return build(mesh, 4, ((0, 768), (768, 640), (1408, 640)), (384, 384, 256))
+    return build(mesh, 4, ((0, 768), (768, 640), (1408, 640)), ((384, 384, 256), (384, 256, 384)))

time: 77.7 us -> 75.2 us (0.968)
  the two profiles are of different devices: /device:TPU:6 before, /device:TPU:1 now
where the time goes in v6:
time: 75.2 us; the launch traced here: 73.8 us
  Pallas kernels  73.1 us (97%)
    pallas_call x1, Pallas kernels, device_step(): pl.pallas_call(functools.partial(moe_kernel, n, parts, lefts), out_shape=...  73.1 us

profile of v6, /device:TPU:1, one launch (start us, length us, event | category | flops | bytes accessed | tf_op | source)
XLA Modules:
  0.0 73.8 jit_solution(17247888488204064032)
XLA Ops:
  0.0 73.1 %moe.1 = bf16[32,2048]{1,0:T(8,128)(2,1)S(1)} custom-call(bf16[32,2048]{1,0:T(8,128)(2,1)} %x_hbm.1, bf16[2048,128]{1,0:T(8,128)(2,1)} %wr_hbm.1, s32[8,32]{1,0:T(8,128)} %bitcast.1, bf16[1,2048,768]{2,1,0:T(8,128)(2,1)} %wg_hbm.1, bf16[1,2048,768]{2,1,0:T(8,128)(2,1)} %wu_hbm.1, bf16[1,768,2048]{2,1,0:T(8,128)(2,1)} %wd_hbm.1), custom_call_target="tpu_custom_call" | custom-call | tf_op jit(solution)/shard_map/moe/pallas_call | solution.py:311
  73.1 0.7 copy.8

commit v7 on v6

--- a/solution.py
+++ b/solution.py
@@ -10,6 +10,7 @@
 F32 = jnp.float32
 BF16 = jnp.bfloat16
 CAP = 8
+PLAN = 'y f0 x3 f1 f2 n0 f3 n1 n2 n3 h0 h1 h2 h3'
 
 
 def _iota(shape, dim):
@@ -92,24 +93,29 @@
         pl.semaphore_signal(barrier, inc=1, device_id={'expert': peer}, device_id_type=pl.DeviceIdType.MESH)
     for load in loads[:3]:
         load.wait()
+    tab_ref[...] = routing_table(x_ref[...], wr_ref[...], rt_ref[...])
+    for p, (off, w) in enumerate(parts):
+        (a, _), (b, _), _ = mine[p]
+        xbuf[p][b, a] = x_ref[:, off:off + w]
+        tbuf[p][b, a] = tab_ref[...]
     pl.semaphore_wait(barrier, len(peers))
 
     near_first, far_first = (1, 3, 2), (2, 1, 3)
 
+    for d in far_first:
+        for p in range(np_):
+            (a, _), (b, _), _ = mine[p]
+            put(tab_ref, tbuf[p].at[b, a], ta_s.at[p], ta_r.at[p], moved(mine[p][0], d))
     for axis, send, recv in ((0, xa_s, xa_r), (1, xb_s, xb_r)):
         for d in far_first:
             for p, (off, w) in enumerate(parts):
                 (a, _), (b, _), _ = mine[p]
                 put(x_ref.at[:, pl.ds(off, w)], xbuf[p].at[b, a], send.at[p], recv.at[p, d - 1], moved(mine[p][axis], d))
-    tab_ref[...] = routing_table(x_ref[...], wr_ref[...], rt_ref[...])
-    for p, (off, w) in enumerate(parts):
-        (a, _), (b, _), _ = mine[p]
-        xbuf[p][b, a] = x_ref[:, off:off + w]
-        tbuf[p][b, a] = tab_ref[...]
-    for d in far_first:
-        for p in range(np_):
-            (a, _), (b, _), _ = mine[p]
-            put(tab_ref, tbuf[p].at[b, a], ta_s.at[p], ta_r.at[p], moved(mine[p][0], d))
+    for p in range(np_):
+        b = mine[p][1][0]
+        drain(tbuf[p].at[0, pl.ds(0, n - 1)], ta_r.at[p])
+        for d in far_first:
+            put(tbuf[p].at[b], tbuf[p].at[b], tb_s.at[p], tb_r.at[p], moved(mine[p][1], d))
     for da in near_first:
         for p in range(np_):
             (a, _), (b, _), _ = mine[p]
@@ -117,11 +123,6 @@
             drain(xbuf[p].at[0, 0], xa_r.at[p, da - 1])
             for d in far_first:
                 put(xbuf[p].at[b, src], xbuf[p].at[b, src], xb_s.at[p], xb_r.at[p, d - 1], moved(mine[p][1], d))
-    for p in range(np_):
-        b = mine[p][1][0]
-        drain(tbuf[p].at[0, pl.ds(0, n - 1)], ta_r.at[p])
-        for d in far_first:
-            put(tbuf[p].at[b], tbuf[p].at[b], tb_s.at[p], tb_r.at[p], moved(mine[p][1], d))
 
     q_order = (4, 5, 2, 3, 6, 7, 1)
 
@@ -224,8 +225,6 @@
                         cbuf[p][bb, aa, k * 2 + core] = obuf[i, z, y, cc, :, off:off + w]
         return carry
 
-    lax.fori_loop(0, n, expert, 0)
-
     def line_sum(p, db, i):
         w = parts[p][1]
         _, (b, _), (k, _) = mine[p]
@@ -270,13 +269,16 @@
             def _():
                 abuf[p][a] = pbuf[p][i]
 
-    for t in range(n + 2):
-        if t < n:
-            far(t)
-        if 0 <= t - 1 < n:
-            near(t - 1)
-        if t >= 2:
-            here(t - 2)
+    steps = {'x': lambda i: expert(i, 0), 'f': far, 'n': near, 'h': here}
+    todo = PLAN.split()
+    if todo[0] == 'x':
+        lax.fori_loop(0, n, expert, 0)
+        todo = todo[1:]
+    elif todo[0] == 'y':
+        lax.fori_loop(0, n - 1, expert, 0)
+        todo = todo[1:]
+    for step in todo:
+        steps[step[0]](int(step[1]))
     for p, (off, w) in enumerate(parts):
         drain(pbuf[p].at[pl.ds(0, n - 1)], ra_r.at[p])
         total = abuf[p][0]

time: 75.2 us -> 70.4 us (0.936); the launches traced: 73.8 us -> 70.3 us
  Pallas kernels: 73.1 us -> 69.6 us
    pallas_call x1, Pallas kernels: 73.1 us -> 69.6 us  [device_step(): pl.pallas_call(functools.partial(moe_kernel, n, parts, lefts), out_shape=...]
where the time goes in v7:
time: 70.4 us; the launch traced here: 70.3 us
  Pallas kernels  69.6 us (99%)
    pallas_call x1, Pallas kernels, device_step(): pl.pallas_call(functools.partial(moe_kernel, n, parts, lefts), out_shape=...  69.6 us

profile of v7, /device:TPU:1, one launch (start us, length us, event | category | flops | bytes accessed | tf_op | source)
XLA Modules:
  0.0 70.3 jit_solution(16122196334637081670)
XLA Ops:
  0.0 69.6 %moe.1 = bf16[32,2048]{1,0:T(8,128)(2,1)S(1)} custom-call(bf16[32,2048]{1,0:T(8,128)(2,1)} %x_hbm.1, bf16[2048,128]{1,0:T(8,128)(2,1)} %wr_hbm.1, s32[8,32]{1,0:T(8,128)} %bitcast.1, bf16[1,2048,768]{2,1,0:T(8,128)(2,1)} %wg_hbm.1, bf16[1,2048,768]{2,1,0:T(8,128)(2,1)} %wu_hbm.1, bf16[1,768,2048]{2,1,0:T(8,128)(2,1)} %wd_hbm.1), custom_call_target="tpu_custom_call" | custom-call | tf_op jit(solution)/shard_map/moe/pallas_call | solution.py:313
  69.6 0.7 copy.8

commit v8 on v7

--- a/solution.py
+++ b/solution.py
@@ -10,7 +10,7 @@
 F32 = jnp.float32
 BF16 = jnp.bfloat16
 CAP = 8
-PLAN = 'y f0 x3 f1 f2 n0 f3 n1 n2 n3 h0 h1 h2 h3'
+RETURN_STEPS = ('f0', 'x3', 'f1', 'f2', 'n0', 'f3', 'n1', 'n2', 'n3', 'h0', 'h1', 'h2', 'h3')
 
 
 def _iota(shape, dim):
@@ -49,8 +49,8 @@
 
 def moe_kernel(n, parts, lefts, x_hbm, wr_hbm, rt_hbm, wg_hbm, wu_hbm, wd_hbm, y_ref, x_ref, wr_ref, rt_ref, wg, wu, wd, rbuf, obuf, tab_ref, *rest):
     np_ = len(parts)
-    tbuf, xbuf, sbuf, cbuf, farp, fari, nearp, neari, pbuf, abuf, mixbuf = [rest[i * np_:(i + 1) * np_] for i in range(11)]
-    (w_sem, ta_s, ta_r, tb_s, tb_r, xa_s, xa_r, xb_s, xb_r, c_s, c_r, rc_s, rc_r, rf_s, rf_r, rn_s, rn_r, ra_s, ra_r) = rest[11 * np_:]
+    tbuf, xbuf, sbuf, cbuf, farp, fari, nearp, neari, pbuf, abuf, mixbuf, ownbuf = [rest[i * np_:(i + 1) * np_] for i in range(12)]
+    (w_sem, ta_s, ta_r, tb_s, tb_r, xa_s, xa_r, xb_s, xb_r, xd_s, xd_r, c_s, c_r, rc_s, rc_r, rf_s, rf_r, rn_s, rn_r, ra_s, ra_r) = rest[12 * np_:]
     tok, width = x_ref.shape
     experts = tab_ref.shape[1]
     me = lax.axis_index('expert')
@@ -101,28 +101,6 @@
     pl.semaphore_wait(barrier, len(peers))
 
     near_first, far_first = (1, 3, 2), (2, 1, 3)
-
-    for d in far_first:
-        for p in range(np_):
-            (a, _), (b, _), _ = mine[p]
-            put(tab_ref, tbuf[p].at[b, a], ta_s.at[p], ta_r.at[p], moved(mine[p][0], d))
-    for axis, send, recv in ((0, xa_s, xa_r), (1, xb_s, xb_r)):
-        for d in far_first:
-            for p, (off, w) in enumerate(parts):
-                (a, _), (b, _), _ = mine[p]
-                put(x_ref.at[:, pl.ds(off, w)], xbuf[p].at[b, a], send.at[p], recv.at[p, d - 1], moved(mine[p][axis], d))
-    for p in range(np_):
-        b = mine[p][1][0]
-        drain(tbuf[p].at[0, pl.ds(0, n - 1)], ta_r.at[p])
-        for d in far_first:
-            put(tbuf[p].at[b], tbuf[p].at[b], tb_s.at[p], tb_r.at[p], moved(mine[p][1], d))
-    for da in near_first:
-        for p in range(np_):
-            (a, _), (b, _), _ = mine[p]
-            src = mod(a + n - da)
-            drain(xbuf[p].at[0, 0], xa_r.at[p, da - 1])
-            for d in far_first:
-                put(xbuf[p].at[b, src], xbuf[p].at[b, src], xb_s.at[p], xb_r.at[p, d - 1], moved(mine[p][1], d))
 
     q_order = (4, 5, 2, 3, 6, 7, 1)
 
@@ -149,9 +127,35 @@
         bb = mod(b + n - db)
         aa = mod(i + 2 * n - bb - k)
         z, y = canon(p, core, aa, bb, k)
-        for q in q_order:
-            put(sbuf[p].at[db, q, aa], rbuf.at[i, z, y, core, :, pl.ds(off, w)], c_s.at[p], c_r.at[p, i], moved(mine[p][2], q // 2, q % 2))
-        rbuf[i, z, y, core, :, off:off + w] = sbuf[p][db, 0, aa]
+
+        def go():
+            for q in q_order:
+                put(sbuf[p].at[db, q, aa], rbuf.at[i, z, y, core, :, pl.ds(off, w)], c_s.at[p], c_r.at[p, i], moved(mine[p][2], q // 2, q % 2))
+            rbuf[i, z, y, core, :, off:off + w] = sbuf[p][db, 0, aa]
+
+        if db:
+            go()
+        else:
+            pl.when(aa != a)(go)
+
+    def own_rows():
+        for p, (off, w) in enumerate(parts):
+            (a, _), (b, _), (k, _) = mine[p]
+            i = mod(a + b + k)
+            table = tab_ref[:CAP]
+            lane = _iota((CAP, experts), 1)
+            token = _iota((CAP, tok), 1).astype(F32)
+            picks = []
+            for q in range(2 * n):
+                col = jnp.sum(jnp.where(lane == moved(mine[p][2], q // 2, q % 2), table, 0.0), axis=1, keepdims=True)
+                picks.append((col == token).astype(F32))
+            pick = jnp.concatenate(picks, axis=0).astype(BF16)
+            rows = jnp.dot(pick, x_ref[:, off:off + w], preferred_element_type=F32).astype(BF16)
+            ownbuf[p][...] = rows.reshape(2 * n, CAP, w)
+            z, y = canon(p, core, a, b, k)
+            for q in q_order:
+                put(ownbuf[p].at[q], rbuf.at[i, z, y, core, :, pl.ds(off, w)], c_s.at[p], c_r.at[p, i], moved(mine[p][2], q // 2, q % 2))
+            rbuf[i, z, y, core, :, off:off + w] = ownbuf[p][0]
 
     def chunk_rows(i, dbs):
         for db in dbs:
@@ -164,17 +168,74 @@
             return carry
         return run
 
+
+    for d in far_first:
+        for p in range(np_):
+            (a, _), (b, _), _ = mine[p]
+            put(tab_ref, tbuf[p].at[b, a], ta_s.at[p], ta_r.at[p], moved(mine[p][0], d))
+    def own_a(d):
+        for p, (off, w) in enumerate(parts):
+            (a, _), (b, _), _ = mine[p]
+            put(x_ref.at[:, pl.ds(off, w)], xbuf[p].at[b, a], xa_s.at[p], xa_r.at[p, d - 1], moved(mine[p][0], d))
+
+    def own_b(side):
+        for p, (off, w) in enumerate(parts):
+            (a, _), (b, _), _ = mine[p]
+            put(x_ref.at[:, pl.ds(off, w)], xbuf[p].at[b, a], xb_s.at[p], xb_r.at[p, side, 0], moved(mine[p][1], 1 + 2 * side))
+    own_a(1)
+    own_a(3)
+    own_b(0)
+    own_b(1)
+    own_a(2)
+    own_rows()
+    for p in range(np_):
+        b = mine[p][1][0]
+        drain(tbuf[p].at[0, pl.ds(0, n - 1)], ta_r.at[p])
+        for d in far_first:
+            put(tbuf[p].at[b], tbuf[p].at[b], tb_s.at[p], tb_r.at[p], moved(mine[p][1], d))
+
+    def along_b(da):
+        for p in range(np_):
+            (a, _), (b, _), _ = mine[p]
+            src = mod(a + n - da)
+            drain(xbuf[p].at[0, 0], xa_r.at[p, da - 1])
+            for side in (0, 1):
+                put(xbuf[p].at[b, src], xbuf[p].at[b, src], xb_s.at[p], xb_r.at[p, side, da], moved(mine[p][1], 1 + 2 * side))
+
+    def onward(da):
+        for side in (0, 1):
+            for p, (off, w) in enumerate(parts):
+                (a, _), (b, _), _ = mine[p]
+                src, bb = mod(a + n - da), mod(b + n - 1 - 2 * side)
+                left = lefts[da % 2][p]
+                drain(xbuf[p].at[0, 0], xb_r.at[p, side, da])
+                half = pl.ds(left, w - left) if side else pl.ds(0, left)
+                put(xbuf[p].at[bb, src, :, half], xbuf[p].at[bb, src, :, half], xd_s.at[p], xd_r.at[p], moved(mine[p][1], 1 + 2 * side))
+
+    along_b(1)
+    along_b(3)
+    onward(0)
+    along_b(2)
+
     for p in range(np_):
         select(p, 0)
-    lax.fori_loop(0, n, body((0,)), 0)
+    lax.fori_loop(0, n - 1, body((0,)), 0)
+    for da in near_first:
+        onward(da)
+    chunk_rows(n - 1, (0,))
     for p in range(np_):
         drain(tbuf[p].at[pl.ds(0, n - 1)], tb_r.at[p])
-    for db in near_first:
-        for p in range(np_):
-            drain(xbuf[p].at[0], xb_r.at[p, db - 1])
+    for db in (1, 3):
+        for p in range(np_):
             select(p, db)
         chunk_rows(0, (db,))
-    lax.fori_loop(1, n, body(near_first), 0)
+    chunk_rows(1, (1, 3))
+    for p in range(np_):
+        drain(xbuf[p].at[0], xd_r.at[p])
+        select(p, 2)
+    chunk_rows(0, (2,))
+    chunk_rows(1, (2,))
+    lax.fori_loop(2, n, body((1, 3, 2)), 0)
 
     cols = 2 * n * CAP
     for p in range(np_):
@@ -270,14 +331,8 @@
                 abuf[p][a] = pbuf[p][i]
 
     steps = {'x': lambda i: expert(i, 0), 'f': far, 'n': near, 'h': here}
-    todo = PLAN.split()
-    if todo[0] == 'x':
-        lax.fori_loop(0, n, expert, 0)
-        todo = todo[1:]
-    elif todo[0] == 'y':
-        lax.fori_loop(0, n - 1, expert, 0)
-        todo = todo[1:]
-    for step in todo:
+    lax.fori_loop(0, n - 1, expert, 0)
+    for step in RETURN_STEPS:
         steps[step[0]](int(step[1]))
     for p, (off, w) in enumerate(parts):
         drain(pbuf[p].at[pl.ds(0, n - 1)], ra_r.at[p])
@@ -289,7 +344,8 @@
         drain(tbuf[p].at[0, pl.ds(0, n - 1)], ta_s.at[p])
         drain(tbuf[p].at[pl.ds(0, n - 1)], tb_s.at[p])
         drain(xbuf[p].at[0, pl.ds(0, n - 1)], xa_s.at[p])
-        drain(xbuf[p].at[pl.ds(0, n - 1)], xb_s.at[p])
+        drain(xbuf[p].at[pl.ds(0, 2)], xb_s.at[p])
+        drain(xbuf[p].at[0], xd_s.at[p])
         drain(sbuf[p].at[:, pl.ds(0, 2 * n - 1)], c_s.at[p])
         drain(cbuf[p].at[:, :, pl.ds(0, 2 * n - 1)], rc_s.at[p])
         drain(farp[p], rf_s.at[p])
@@ -330,8 +386,9 @@
                 *[pltpu.VMEM((n, tok, w), F32) for _, w in parts],
                 *[pltpu.VMEM((n, tok, w), F32) for _, w in parts],
                 *[pltpu.VMEM((n, n, 3 * tok, cols), BF16) for _ in parts],
+                *[pltpu.VMEM((2 * n, CAP, w), BF16) for _, w in parts],
                 dma((6,)), dma((np_,)), dma((np_,)), dma((np_,)), dma((np_,)),
-                dma((np_,)), dma((np_, n - 1)), dma((np_,)), dma((np_, n - 1)), dma((np_,)), dma((np_, n)),
+                dma((np_,)), dma((np_, n - 1)), dma((np_,)), dma((np_, 2, n)), dma((np_,)), dma((np_,)), dma((np_,)), dma((np_, n)),
                 dma((np_,)), dma((np_, n, n)), dma((np_,)), dma((np_, n)), dma((np_,)), dma((np_, n)), dma((np_,)), dma((np_,)),
             ],
             compiler_params=pltpu.CompilerParams(collective_id=0, has_side_effects=True, vmem_limit_bytes=57 * 1024 * 1024),

time: 70.4 us -> 68.6 us (0.974)
  Pallas kernels: 69.6 us -> 67.8 us
    pallas_call x1, Pallas kernels: 69.6 us -> 67.8 us  [device_step(): pl.pallas_call(functools.partial(moe_kernel, n, parts, lefts), out_shape=...]
where the time goes in v8:
time: 68.6 us; the launch traced here: 68.5 us
  Pallas kernels  67.8 us (99%)
    pallas_call x1, Pallas kernels, device_step(): pl.pallas_call(functools.partial(moe_kernel, n, parts, lefts), out_shape=...  67.8 us

profile of v8, /device:TPU:1, one launch (start us, length us, event | category | flops | bytes accessed | tf_op | source)
XLA Modules:
  0.0 68.5 jit_solution(511710043160253512)
XLA Ops:
  0.0 67.8 %moe.1 = bf16[32,2048]{1,0:T(8,128)(2,1)S(1)} custom-call(bf16[32,2048]{1,0:T(8,128)(2,1)} %x_hbm.1, bf16[2048,128]{1,0:T(8,128)(2,1)} %wr_hbm.1, s32[8,32]{1,0:T(8,128)} %bitcast.1, bf16[1,2048,768]{2,1,0:T(8,128)(2,1)} %wg_hbm.1, bf16[1,2048,768]{2,1,0:T(8,128)(2,1)} %wu_hbm.1, bf16[1,768,2048]{2,1,0:T(8,128)(2,1)} %wd_hbm.1), custom_call_target="tpu_custom_call" | custom-call | tf_op jit(solution)/shard_map/moe/pallas_call | solution.py:369
  67.8 0.7 copy.8

commit v9 on v8

--- a/solution.py
+++ b/solution.py
@@ -24,35 +24,43 @@
 def routing_table(x, wr, routes_t):
     tok, experts = x.shape[0], wr.shape[1]
     top_k = routes_t.shape[0]
-    logits = jnp.dot(x, wr, preferred_element_type=F32)
-    eye = (_iota((top_k, top_k), 0) == _iota((top_k, top_k), 1)).astype(BF16)
-    routes = lax.dot_general(routes_t.astype(F32).astype(BF16), eye, (((0,), (0,)), ((), ())), preferred_element_type=F32)
-    lane = _iota((tok, experts), 1).astype(F32)
-    hit = jnp.zeros((tok, experts), F32)
-    for j in range(top_k):
-        hit += (routes[:, j:j + 1] == lane).astype(F32)
+    logits = jnp.dot(x, wr, preferred_element_type=F32).T
+    ident = _iota((experts, tok), 0)
+    chosen = [ident == routes_t[j:j + 1] for j in range(top_k)]
+    hit = jnp.zeros((experts, tok), F32)
+    for c in chosen:
+        hit += c.astype(F32)
     on = hit > 0.5
-    top = jnp.max(jnp.where(on, logits, -jnp.inf), axis=1, keepdims=True)
+    top = jnp.max(jnp.where(on, logits, -jnp.inf), axis=0, keepdims=True)
     e = jnp.where(on, jnp.exp(jnp.where(on, logits, top) - top), 0.0)
-    gate = e / jnp.sum(e, axis=1, keepdims=True)
-    below = (_iota((tok, tok), 1) < _iota((tok, tok), 0)).astype(BF16)
-    rank = jnp.dot(below, hit.astype(BF16), preferred_element_type=F32)
-    rank = jnp.where(on, rank, -1.0)
-    row = _iota((tok, experts), 0).astype(F32)
-    toks, gates = [], []
-    for r in range(CAP):
-        at = rank == r
-        toks.append(jnp.sum(jnp.where(at, row + 1.0, 0.0), axis=0, keepdims=True) - 1.0)
-        gates.append(jnp.sum(jnp.where(at, gate, 0.0), axis=0, keepdims=True))
-    return jnp.concatenate(toks + gates, axis=0)
+    gate = e / jnp.sum(e, axis=0, keepdims=True)
+    above = (_iota((tok, tok), 0) < _iota((tok, tok), 1)).astype(BF16)
+    slot = jnp.dot(hit.astype(BF16), above, preferred_element_type=F32)
+    pick = lambda c, v: jnp.sum(jnp.where(c, v, 0.0), axis=0, keepdims=True)
+    codes = [routes_t[j:j + 1].astype(F32) * CAP + pick(chosen[j], slot) for j in range(top_k)]
+    return jnp.concatenate(codes + [pick(c, gate) for c in chosen], axis=0)
+
+
+def split3(v):
+    v1 = v.astype(BF16).astype(F32)
+    v2 = (v - v1).astype(BF16).astype(F32)
+    return v1, v2, v - v1 - v2
+
+
+def one_hot(codes, want):
+    out = jnp.zeros((want.shape[0], codes.shape[1]), F32)
+    for j in range(codes.shape[0]):
+        out += (codes[j:j + 1] == want).astype(F32)
+    return out
 
 
 def moe_kernel(n, parts, lefts, x_hbm, wr_hbm, rt_hbm, wg_hbm, wu_hbm, wd_hbm, y_ref, x_ref, wr_ref, rt_ref, wg, wu, wd, rbuf, obuf, tab_ref, *rest):
+    top_k = rt_ref.shape[0]
     np_ = len(parts)
-    tbuf, xbuf, sbuf, cbuf, farp, fari, nearp, neari, pbuf, abuf, mixbuf, ownbuf = [rest[i * np_:(i + 1) * np_] for i in range(12)]
-    (w_sem, ta_s, ta_r, tb_s, tb_r, xa_s, xa_r, xb_s, xb_r, xd_s, xd_r, c_s, c_r, rc_s, rc_r, rf_s, rf_r, rn_s, rn_r, ra_s, ra_r) = rest[12 * np_:]
+    tbuf, xbuf, sbuf, cbuf, farp, fari, nearp, neari, pbuf, abuf, mixbuf, ownbuf, tline = [rest[i * np_:(i + 1) * np_] for i in range(13)]
+    (w_sem, ta_s, ta_r, tb_s, tb_r, xa_s, xa_r, xb_s, xb_r, xd_s, xd_r, c_s, c_r, rc_s, rc_r, rf_s, rf_r, rn_s, rn_r, ra_s, ra_r) = rest[13 * np_:]
     tok, width = x_ref.shape
-    experts = tab_ref.shape[1]
+    experts = wr_ref.shape[1]
     me = lax.axis_index('expert')
     strides = (2 * n * n, 2 * n, 2)
     pos = tuple(lax.rem(me // s, n) for s in strides)
@@ -94,10 +102,13 @@
     for load in loads[:3]:
         load.wait()
     tab_ref[...] = routing_table(x_ref[...], wr_ref[...], rt_ref[...])
+    terms = jnp.concatenate(split3(tab_ref[...]), axis=0).astype(BF16)
     for p, (off, w) in enumerate(parts):
         (a, _), (b, _), _ = mine[p]
         xbuf[p][b, a] = x_ref[:, off:off + w]
-        tbuf[p][b, a] = tab_ref[...]
+        place = (_iota((tok, n * tok), 1) == _iota((tok, n * tok), 0) + a * tok).astype(BF16)
+        wide = jnp.dot(terms, place, preferred_element_type=F32)
+        tline[p][a] = wide[:2 * top_k] + wide[2 * top_k:4 * top_k] + wide[4 * top_k:]
     pl.semaphore_wait(barrier, len(peers))
 
     near_first, far_first = (1, 3, 2), (2, 1, 3)
@@ -108,16 +119,11 @@
         off, w = parts[p]
         (a, _), (b, _), (k, _) = mine[p]
         bb = mod(b + n - db)
-        table = tbuf[p][bb][:, :CAP].reshape(n * CAP, experts)
-        shift = (_iota((n * CAP, 1), 0) // CAP * tok).astype(F32)
-        lane = _iota((n * CAP, experts), 1)
-        token = _iota((n * CAP, n * tok), 1).astype(F32)
-        picks = []
-        for q in range(2 * n):
-            col = jnp.sum(jnp.where(lane == moved(mine[p][2], q // 2, q % 2), table, 0.0), axis=1, keepdims=True)
-            want = jnp.where(col >= 0.0, col + shift, -1.0)
-            picks.append((want == token).astype(F32))
-        pick = jnp.concatenate(picks, axis=0).astype(BF16)
+        row = _iota((n * CAP, 1), 0)
+        want = jnp.concatenate([(moved(mine[p][2], q // 2, q % 2) * CAP + lax.rem(row, CAP)).astype(F32) for q in range(2 * n)], axis=0)
+        shape = (2 * n * n * CAP, n * tok)
+        same = lax.rem(_iota(shape, 0) // CAP, n) == _iota(shape, 1) // tok
+        pick = jnp.where(same, one_hot(tbuf[p][bb, :top_k], want), 0.0).astype(BF16)
         rows = jnp.dot(pick, xbuf[p][bb].reshape(n * tok, w), preferred_element_type=F32).astype(BF16)
         sbuf[p][db] = rows.reshape(2 * n, n, CAP, w)
 
@@ -142,14 +148,9 @@
         for p, (off, w) in enumerate(parts):
             (a, _), (b, _), (k, _) = mine[p]
             i = mod(a + b + k)
-            table = tab_ref[:CAP]
-            lane = _iota((CAP, experts), 1)
-            token = _iota((CAP, tok), 1).astype(F32)
-            picks = []
-            for q in range(2 * n):
-                col = jnp.sum(jnp.where(lane == moved(mine[p][2], q // 2, q % 2), table, 0.0), axis=1, keepdims=True)
-                picks.append((col == token).astype(F32))
-            pick = jnp.concatenate(picks, axis=0).astype(BF16)
+            row = _iota((CAP, 1), 0)
+            want = jnp.concatenate([(moved(mine[p][2], q // 2, q % 2) * CAP + row).astype(F32) for q in range(2 * n)], axis=0)
+            pick = one_hot(tab_ref[:top_k], want).astype(BF16)
             rows = jnp.dot(pick, x_ref[:, off:off + w], preferred_element_type=F32).astype(BF16)
             ownbuf[p][...] = rows.reshape(2 * n, CAP, w)
             z, y = canon(p, core, a, b, k)
@@ -172,7 +173,7 @@
     for d in far_first:
         for p in range(np_):
             (a, _), (b, _), _ = mine[p]
-            put(tab_ref, tbuf[p].at[b, a], ta_s.at[p], ta_r.at[p], moved(mine[p][0], d))
+            put(tline[p].at[a], tline[p].at[a], ta_s.at[p], ta_r.at[p], moved(mine[p][0], d))
     def own_a(d):
         for p, (off, w) in enumerate(parts):
             (a, _), (b, _), _ = mine[p]
@@ -190,7 +191,11 @@
     own_rows()
     for p in range(np_):
         b = mine[p][1][0]
-        drain(tbuf[p].at[0, pl.ds(0, n - 1)], ta_r.at[p])
+        drain(tline[p].at[pl.ds(0, n - 1)], ta_r.at[p])
+        line = tline[p][0]
+        for i in range(1, n):
+            line += tline[p][i]
+        tbuf[p][b] = line
         for d in far_first:
             put(tbuf[p].at[b], tbuf[p].at[b], tb_s.at[p], tb_r.at[p], moved(mine[p][1], d))
 
@@ -240,22 +245,19 @@
     cols = 2 * n * CAP
     for p in range(np_):
         (a, sa), (b, sb), (_, sc) = mine[p]
-        slot = _iota((experts, cols), 1)
+        slot = _iota((cols, 1), 0)
         ident = slot // (2 * CAP) * sc + lax.rem(slot // CAP, 2) + a * sa + b * sb
-        spread = (ident == _iota((experts, cols), 0)).astype(BF16)
-        keep = _iota((CAP, cols), 0) == lax.rem(_iota((CAP, cols), 1), CAP)
+        want = (ident * CAP + lax.rem(slot, CAP)).astype(F32)
         for bb in range(n):
-            tg = tbuf[p][bb]
-            gate = tg[:, CAP:]
-            g1 = gate.astype(BF16).astype(F32)
-            g2 = (gate - g1).astype(BF16).astype(F32)
-            g3 = gate - g1 - g2
-            terms = jnp.concatenate([tg[:, :CAP], g1, g2, g3], axis=1).reshape(n * 4 * CAP, experts).astype(BF16)
-            wide = jnp.dot(terms, spread, preferred_element_type=F32)
+            tb = tbuf[p][bb]
+            gates = split3(tb[top_k:])
+            mix = [jnp.zeros((cols, n * tok), F32) for _ in gates]
+            for j in range(top_k):
+                at = tb[j:j + 1] == want
+                mix = [m + jnp.where(at, g[j:j + 1], 0.0) for m, g in zip(mix, gates)]
+            mix = [m.T for m in mix]
             for aa in range(n):
-                line = [jnp.sum(jnp.where(keep, wide[(aa * 4 + i) * CAP:(aa * 4 + i + 1) * CAP], 0.0), axis=0, keepdims=True) for i in range(4)]
-                here = line[0] == _iota((tok, cols), 0).astype(F32)
-                mixbuf[p][bb, aa] = jnp.concatenate([jnp.where(here, line[i], 0.0) for i in (1, 2, 3)], axis=0).astype(BF16)
+                mixbuf[p][bb, aa] = jnp.concatenate([m[aa * tok:(aa + 1) * tok] for m in mix], axis=0).astype(BF16)
 
     for load in loads[3:]:
         load.wait()
@@ -341,7 +343,7 @@
             total += abuf[p][i]
         y_ref[:, off:off + w] = total.astype(BF16)
     for p in range(np_):
-        drain(tbuf[p].at[0, pl.ds(0, n - 1)], ta_s.at[p])
+        drain(tline[p].at[pl.ds(0, n - 1)], ta_s.at[p])
         drain(tbuf[p].at[pl.ds(0, n - 1)], tb_s.at[p])
         drain(xbuf[p].at[0, pl.ds(0, n - 1)], xa_s.at[p])
         drain(xbuf[p].at[pl.ds(0, 2)], xb_s.at[p])
@@ -374,8 +376,8 @@
                 pltpu.VMEM((tok, width), BF16), pltpu.VMEM((width, experts), BF16), pltpu.VMEM((routes.shape[1], tok), jnp.int32),
                 pltpu.VMEM((width, ff), BF16), pltpu.VMEM((width, ff), BF16), pltpu.VMEM((ff, width), BF16),
                 pltpu.VMEM((n, n, n, 2, CAP, width), BF16), pltpu.VMEM((n, n, n, 2, CAP, width), BF16),
-                pltpu.VMEM((2 * CAP, experts), F32),
-                *[pltpu.VMEM((n, n, 2 * CAP, experts), F32) for _ in parts],
+                pltpu.VMEM((2 * routes.shape[1], tok), F32),
+                *[pltpu.VMEM((n, 2 * routes.shape[1], n * tok), F32) for _ in parts],
                 *[pltpu.VMEM((n, n, tok, w), BF16) for _, w in parts],
                 *[pltpu.VMEM((n, 2 * n, n, CAP, w), BF16) for _, w in parts],
                 *[pltpu.VMEM((n, n, 2 * n, CAP, w), BF16) for _, w in parts],
@@ -387,6 +389,7 @@
                 *[pltpu.VMEM((n, tok, w), F32) for _, w in parts],
                 *[pltpu.VMEM((n, n, 3 * tok, cols), BF16) for _ in parts],
                 *[pltpu.VMEM((2 * n, CAP, w), BF16) for _, w in parts],
+                *[pltpu.VMEM((n, 2 * routes.shape[1], n * tok), F32) for _ in parts],
                 dma((6,)), dma((np_,)), dma((np_,)), dma((np_,)), dma((np_,)),
                 dma((np_,)), dma((np_, n - 1)), dma((np_,)), dma((np_, 2, n)), dma((np_,)), dma((np_,)), dma((np_,)), dma((np_, n)),
                 dma((np_,)), dma((np_, n, n)), dma((np_,)), dma((np_, n)), dma((np_,)), dma((np_, n)), dma((np_,)), dma((np_,)),

time: 68.6 us -> 68.1 us (level)
  no operation moved by 1% of the time
where the time goes in v9:
time: 68.1 us; the launch traced here: 68 us
  Pallas kernels  67.3 us (99%)
    pallas_call x1, Pallas kernels, device_step(): pl.pallas_call(functools.partial(moe_kernel, n, parts, lefts), out_shape=...  67.3 us

profile of v9, /device:TPU:1, one launch (start us, length us, event | category | flops | bytes accessed | tf_op | source)
XLA Modules:
  0.0 68.0 jit_solution(16900354414799907449)
XLA Ops:
  0.0 67.3 %moe.1 = bf16[32,2048]{1,0:T(8,128)(2,1)S(1)} custom-call(bf16[32,2048]{1,0:T(8,128)(2,1)} %x_hbm.1, bf16[2048,128]{1,0:T(8,128)(2,1)} %wr_hbm.1, s32[8,32]{1,0:T(8,128)} %bitcast.1, bf16[1,2048,768]{2,1,0:T(8,128)(2,1)} %wg_hbm.1, bf16[1,2048,768]{2,1,0:T(8,128)(2,1)} %wu_hbm.1, bf16[1,768,2048]{2,1,0:T(8,128)(2,1)} %wd_hbm.1), custom_call_target="tpu_custom_call" | custom-call | tf_op jit(solution)/shard_map/moe/pallas_call | solution.py:371
  67.3 0.7 copy.8

commit v10 on v9

--- a/solution.py
+++ b/solution.py
@@ -113,7 +113,7 @@
 
     near_first, far_first = (1, 3, 2), (2, 1, 3)
 
-    q_order = (4, 5, 2, 3, 6, 7, 1)
+    q_order = (1, 4, 5, 2, 3, 6, 7)
 
     def select(p, db):
         off, w = parts[p]
@@ -233,8 +233,7 @@
     for db in (1, 3):
         for p in range(np_):
             select(p, db)
-        chunk_rows(0, (db,))
-    chunk_rows(1, (1, 3))
+    lax.fori_loop(0, 2, body((1, 3)), 0)
     for p in range(np_):
         drain(xbuf[p].at[0], xd_r.at[p])
         select(p, 2)
@@ -318,11 +317,12 @@
 
     def here(i):
         for p in range(np_):
+            pbuf[p][i] = line_sum(p, 0, i)
+        for p in range(np_):
             (a, sa), (b, _), (k, _) = mine[p]
             aa = mod(i + 2 * n - b - k)
-            own = line_sum(p, 0, i)
             drain(neari[p].at[i], rn_r.at[p, i])
-            pbuf[p][i] = own + neari[p][i, 0] + neari[p][i, 1]
+            pbuf[p][i] += neari[p][i, 0] + neari[p][i, 1]
 
             @pl.when(aa != a)
             def _():

time: 68.1 us -> 67.7 us (level)
  no operation moved by 1% of the time
where the time goes in v10:
time: 67.7 us; the launch traced here: 67.6 us
  Pallas kernels  67 us (99%)
    pallas_call x1, Pallas kernels, device_step(): pl.pallas_call(functools.partial(moe_kernel, n, parts, lefts), out_shape=...  67 us

profile of v10, /device:TPU:1, one launch (start us, length us, event | category | flops | bytes accessed | tf_op | source)
XLA Modules:
  0.0 67.6 jit_solution(1045172604138569912)
XLA Ops:
  0.0 67.0 %moe.1 = bf16[32,2048]{1,0:T(8,128)(2,1)S(1)} custom-call(bf16[32,2048]{1,0:T(8,128)(2,1)} %x_hbm.1, bf16[2048,128]{1,0:T(8,128)(2,1)} %wr_hbm.1, s32[8,32]{1,0:T(8,128)} %bitcast.1, bf16[1,2048,768]{2,1,0:T(8,128)(2,1)} %wg_hbm.1, bf16[1,2048,768]{2,1,0:T(8,128)(2,1)} %wu_hbm.1, bf16[1,768,2048]{2,1,0:T(8,128)(2,1)} %wd_hbm.1), custom_call_target="tpu_custom_call" | custom-call | tf_op jit(solution)/shard_map/moe/pallas_call | solution.py:371
  67.0 0.7 copy.8

commit v11 on v10

--- a/solution.py
+++ b/solution.py
@@ -237,7 +237,7 @@
     for p in range(np_):
         drain(xbuf[p].at[0], xd_r.at[p])
         select(p, 2)
-    chunk_rows(0, (2,))
+        send_rows(p, 2, 0)
     chunk_rows(1, (2,))
     lax.fori_loop(2, n, body((1, 3, 2)), 0)
 

time: 67.7 us -> 67.8 us (level)
  no operation moved by 1% of the time
where the time goes in v11:
time: 67.8 us; the launch traced here: 67.7 us
  Pallas kernels  67 us (99%)
    pallas_call x1, Pallas kernels, device_step(): pl.pallas_call(functools.partial(moe_kernel, n, parts, lefts), out_shape=...  67 us

profile of v11, /device:TPU:1, one launch (start us, length us, event | category | flops | bytes accessed | tf_op | source)
XLA Modules:
  0.0 67.7 jit_solution(12038984376135045637)
XLA Ops:
  0.0 67.0 %moe.1 = bf16[32,2048]{1,0:T(8,128)(2,1)S(1)} custom-call(bf16[32,2048]{1,0:T(8,128)(2,1)} %x_hbm.1, bf16[2048,128]{1,0:T(8,128)(2,1)} %wr_hbm.1, s32[8,32]{1,0:T(8,128)} %bitcast.1, bf16[1,2048,768]{2,1,0:T(8,128)(2,1)} %wg_hbm.1, bf16[1,2048,768]{2,1,0:T(8,128)(2,1)} %wu_hbm.1, bf16[1,768,2048]{2,1,0:T(8,128)(2,1)} %wd_hbm.1), custom_call_target="tpu_custom_call" | custom-call | tf_op jit(solution)/shard_map/moe/pallas_call | solution.py:371
  67.0 0.7 copy.8
